TPU v7x, 512 devices: a whole 4x8x8 slice. The times are simulated.
512 devices in a mesh: role: 4 (over z_lo, core), grp: 32 (over z_hi, y), rep: 4 (over x).
Axes of the slice: x: 4, y: 8, z: 8 (z_hi: 4, z_lo: 2; z = z_hi * 2 + z_lo), core: 2. Of those that a mesh axis runs over, the one named last changes fastest.
Arguments:
- facets: bfloat16 [4, 2, 4096, 4096], P('role', None, ('grp', 'rep')), may hold values from -6 to 6
- taper: float32 [4, 4096], P('role'), may hold values from 0.3 to 1.5
- kernel: float32 [8], replicated, may hold values from 0.1 to 0.5
- observed: float32 [2, 128, 16, 512], P(None, ('role', 'grp'), 'rep'), may hold values from -6 to 6
- patch_pos: int32 [128, 16], P(('role', 'grp'), 'rep'), may hold values from 0 to 23, as said below
- counts: int32 [128, 16], P(('role', 'grp'), 'rep'), may hold values from 1 to 512, 5120 in all within a row
- vis_u: int32 [128, 16, 512], P(('role', 'grp'), 'rep'), may hold values from 0 to 24
- vis_v: int32 [128, 16, 512], P(('role', 'grp'), 'rep'), may hold values from 0 to 24
Outputs:
- residual_vis: float32 [2, 128, 16, 512], P(None, ('role', 'grp'), 'rep')
- returned: bfloat16 [2, 128, 128, 128], P(None, None, ('grp', 'rep'))
Inputs may be any that keep to these rules, and one draw needn't show every extreme that they name: Visibility slots v < counts are live, the rest are padding; the counts of one subgrid's patches sum to 5120 and one of them equals 512. `patch_pos`: split the patches of a subgrid into 4 aligned runs of 4; in each run the first patch covers a block in the first column of blocks and the second a block in the last column of blocks, the others any block.
All inputs are finite; a program needn't handle non-finite values. No bound on the sum of `counts` on one device may be relied on, other than what follows from the above.
Results may differ from a plain program's by a relative error of at most 0.014.
Values may be sent and summed in bfloat16 or wider, within the bound.
A program may use at most 64 MiB of HBM per device.

v0:
```python
import math

import jax
import jax.numpy as jnp
from jax import lax
from jax.sharding import Mesh
from jax.sharding import PartitionSpec as P

F = 4096
C = 128
PATCH = 32
EDGE = 32
KW = 8
ROLE = ("role_0", "role_1")
ROLE_GRP = ("role_0", "role_1", "grp")


def joined_along(blocks, dim):
    dims = list(blocks.shape[1:])
    dims[dim] *= blocks.shape[0]
    return jnp.moveaxis(blocks, 0, dim).reshape(dims)


def sent_to_all(value, axis):
    copies = jnp.broadcast_to(value, (lax.axis_size(axis), *value.shape))
    return lax.all_to_all(copies, axis, split_axis=0, concat_axis=0, tiled=True)


def gather_directly(value, axis, dim):
    return joined_along(sent_to_all(value, axis), dim)


def extended(value, sides, width):
    edges = {}
    for axis, dim in sides:
        size, length = (lax.axis_size(axis), value.shape[dim])
        up = [(i, (i + 1) % size) for i in range(size - 1)]
        last = lax.slice_in_dim(value, length - width, length, axis=dim)
        leading = lax.slice_in_dim(value, 0, width, axis=dim)
        edges[dim] = (
            lax.ppermute(last, axis, up),
            lax.ppermute(leading, axis, [(b, a) for a, b in up]),
        )
    done = []
    for _, dim in sides:
        low, high = edges[dim]
        around = [(width, width) if d in done else (0, 0) for d in range(value.ndim)]
        value = jnp.concatenate([jnp.pad(low, around), value, jnp.pad(high, around)], axis=dim)
        done.append(dim)
    return value


def shifted(value, axis, by):
    size = lax.axis_size(axis)
    pairs = [(i, i + by) for i in range(size) if 0 <= i + by < size]
    return lax.ppermute(value, axis, pairs)


def gather_in_order(value, axes, turns):
    blocks = value[None]
    for k in turns:
        blocks = lax.all_gather(blocks, axes[k], axis=0, tiled=True)
    carried = [lax.axis_size(axes[k]) for k in reversed(turns)]
    blocks = blocks.reshape(*carried, *value.shape)
    turned = sorted(range(len(turns)), key=lambda place: turns[len(turns) - 1 - place])
    return blocks.transpose(*turned, *range(len(turns), blocks.ndim)).reshape(-1, *value.shape)


def gathered_by_axis(value, axes, turns, dim):
    return joined_along(gather_in_order(value, axes, turns), dim)


def phases(frequency, length):
    columns = jnp.arange(length, dtype=jnp.int32)
    product = frequency[:, None] * columns[None, :] % length
    angles = product.astype(jnp.float32) * (2.0 * math.pi / length)
    return (jnp.cos(angles), jnp.sin(angles))


def windowed(frequency, window):
    length = window.shape[0]
    wave_cos, wave_sin = phases(frequency, length)
    scale_norm = 1.0 / math.sqrt(length)
    table_re = (window[None, :] * wave_cos * scale_norm).astype(jnp.bfloat16)
    table_im = (-(window[None, :] * wave_sin) * scale_norm).astype(jnp.bfloat16)
    return (table_re, table_im)


def contract(left, right):
    return lax.dot_general(
        left, right, (((1,), (1,)), ((), ())), preferred_element_type=jnp.float32
    )


def project(table_re, table_im, data_re, data_im):
    part_re = contract(table_re, data_re) - contract(table_im, data_im)
    part_im = contract(table_re, data_im) + contract(table_im, data_re)
    return (part_re, part_im)


def modulate(part_re, part_im, wave_cos, wave_sin):
    mod_re = (part_re * wave_cos + part_im * wave_sin).astype(jnp.bfloat16)
    mod_im = (part_im * wave_cos - part_re * wave_sin).astype(jnp.bfloat16)
    return (mod_re, mod_im)


def kernel_rows(offsets, kernel):
    cell_index = jnp.arange(PATCH, dtype=jnp.int32)
    distance = cell_index[None, :, None] - offsets[:, None, :]
    result = jnp.zeros(distance.shape, jnp.float32)
    for position in range(KW):
        result = result + kernel[position] * (distance == position).astype(jnp.float32)
    return result


def degrid(widened, patch_pos, counts, vis_u, vis_v, observed, kernel):
    row_blocks = widened.shape[1] // PATCH
    col_blocks = widened.shape[2] // PATCH
    blocks = widened.reshape(2, row_blocks, PATCH, col_blocks, PATCH).transpose(0, 1, 3, 2, 4)
    blocks = blocks.reshape(2, row_blocks * col_blocks, PATCH, PATCH)
    selected = jnp.take(blocks, patch_pos, axis=1).astype(jnp.float32)
    rows_u = kernel_rows(vis_u, kernel)
    rows_v = kernel_rows(vis_v, kernel)
    partial_value = jnp.einsum("cpab,pav->cpbv", selected, rows_u)
    predicted = jnp.einsum("cpbv,pbv->cpv", partial_value, rows_v)
    live_mask = (jnp.arange(observed.shape[-1], dtype=jnp.int32)[None, :] < counts[:, None]).astype(
        jnp.float32
    )
    residual = (observed - predicted) * live_mask[None]
    weighted = residual[:, :, None, :] * rows_v[None]
    gridded = jnp.einsum("pav,cpbv->cpab", rows_u, weighted)
    one_hot = (
        patch_pos[:, None] == jnp.arange(row_blocks * col_blocks, dtype=jnp.int32)[None, :]
    ).astype(jnp.float32)
    placed = jnp.einsum("pq,cpab->cqab", one_hot, gridded)
    regrid = placed.reshape(2, row_blocks, col_blocks, PATCH, PATCH).transpose(0, 1, 3, 2, 4)
    return (residual, regrid.reshape(2, widened.shape[1], widened.shape[2]))


def local(facets, taper, kernel, observed, patch_pos, counts, vis_u, vis_v):
    grp_count = lax.axis_size("grp")
    rep_count = lax.axis_size("rep")
    role_count = lax.axis_size(ROLE)
    sub_cols = role_count * grp_count
    row_share = C // (grp_count * rep_count)
    strip_data = facets[0]
    window = taper[0]
    row_freq = jnp.arange(C, dtype=jnp.int32)
    table_re, table_im = windowed(row_freq, window)
    part_re, part_im = project(table_re, table_im, strip_data[0], strip_data[1])
    partial_value = jnp.stack([part_re, part_im]).astype(jnp.bfloat16)
    row_block = lax.all_to_all(
        partial_value, ("grp", "rep"), split_axis=1, concat_axis=2, tiled=True
    )
    shift_freq = jnp.arange(sub_cols, dtype=jnp.int32) * (F // sub_cols)
    wave_cos, wave_sin = phases(shift_freq, F)
    mod_re, mod_im = modulate(
        row_block[0][None].astype(jnp.float32),
        row_block[1][None].astype(jnp.float32),
        (window[None, :] * wave_cos)[:, None, :],
        (window[None, :] * wave_sin)[:, None, :],
    )
    base_re, base_im = windowed(jnp.arange(C, dtype=jnp.int32), jnp.ones((F,), jnp.float32))
    q_re, q_im = project(
        mod_re.reshape(sub_cols * row_share, F),
        mod_im.reshape(sub_cols * row_share, F),
        base_re,
        base_im,
    )
    contrib = jnp.stack([q_re, q_im]).astype(jnp.bfloat16).reshape(2, sub_cols, row_share, C)
    arrived = lax.all_to_all(contrib, ROLE_GRP, split_axis=1, concat_axis=2, tiled=True)
    arrived = arrived.reshape(2, role_count, grp_count, row_share, C).astype(jnp.float32)
    quarter = jnp.sum(arrived, axis=1).astype(jnp.bfloat16)
    collected_rows = gather_directly(quarter[:, :, None], "rep", 2)
    subgrid = collected_rows.reshape(2, C, C)
    widened = extended(subgrid, ((ROLE_GRP, 2),), EDGE)
    residual, regrid = degrid(
        widened, patch_pos[0], counts[0], vis_u[0], vis_v[0], observed[:, 0], kernel
    )
    left_part = regrid[:, :, :EDGE]
    right_part = regrid[:, :, EDGE + C :]
    center = regrid[:, :, EDGE : EDGE + C]
    from_right = shifted(left_part.astype(jnp.bfloat16), ROLE_GRP, -1).astype(left_part.dtype)
    from_left = shifted(right_part.astype(jnp.bfloat16), ROLE_GRP, 1).astype(right_part.dtype)
    resid = center.at[:, :, :EDGE].add(from_left).at[:, :, C - EDGE :].add(from_right)
    pieces = resid.reshape(2, grp_count * rep_count, row_share, C)
    spread = lax.all_to_all(
        pieces.astype(jnp.bfloat16), ("grp", "rep"), split_axis=1, concat_axis=1, tiled=True
    ).astype(pieces.dtype)
    owned = jnp.sum(spread.reshape(2, grp_count, rep_count, row_share, C), axis=2).astype(
        jnp.bfloat16
    )
    returned = gathered_by_axis(owned, ("role_0", "role_1"), (0, 1), 1)
    return (residual[:, None], returned)


def solution(mesh):
    finer = Mesh(
        mesh.devices.reshape(2, 2, mesh.shape["grp"], mesh.shape["rep"]),
        ("role_0", "role_1", "grp", "rep"),
    )
    placed = (
        P(ROLE, None, ("grp", "rep"), None),
        P(ROLE, None),
        P(),
        P(None, ROLE_GRP, "rep", None),
        P(ROLE_GRP, "rep"),
        P(ROLE_GRP, "rep"),
        P(ROLE_GRP, "rep", None),
        P(ROLE_GRP, "rep", None),
    )
    return jax.shard_map(
        local,
        mesh=finer,
        in_specs=placed,
        out_specs=(P(None, ROLE_GRP, "rep", None), P(None, None, ("grp", "rep"), None)),
        check_vma=False,
    )
```

profile of v0, /device:TPU:1, one launch (start us, length us, event | category | flops | bytes accessed | tf_op | source)
XLA Modules:
  0.0 246.2 jit_solution(7901872494506689286)
XLA Ops:
  0.6 9.8 %fusion.26 = f32[128,32]{0,1:T(8,128)S(1)} fusion(f32[4096]{0:T(1024)} %bitcast.130, bf16[1,2,32,4096]{3,2,1,0:T(8,128)(2,1)} %param.12), kind=kOutput, calls=%fused_computation.48 | convolution fusion | flops 42467328 | bytes 294912 | tf_op jit(solution)/shard_map/dot_general | solution.py:90
  10.5 8.1 %fusion.27 = f32[128,32]{0,1:T(8,128)S(1)} fusion(f32[4096]{0:T(1024)S(1)} %bitcast.131, bf16[1,2,32,4096]{3,2,1,0:T(8,128)(2,1)S(1)} %copy-done.6), kind=kOutput, calls=%fused_computation.49 | convolution fusion | flops 42467328 | bytes 294912 | tf_op jit(solution)/shard_map/dot_general | solution.py:90
  18.6 8.4 %fusion.20 = bf16[1,128,32]{1,2,0:T(8,128)(2,1)S(1)} fusion(f32[128,32]{0,1:T(8,128)S(1)} %fusion.26, f32[4096]{0:T(1024)S(1)} %bitcast.132, bf16[1,2,32,4096]{3,2,1,0:T(8,128)(2,1)S(1)} %copy-done.6), kind=kOutput, calls=%fused_computation.42 | convolution fusion | flops 42999808 | bytes 303104 | tf_op jit(solution)/shard_map/dot_general | solution.py:90
  27.0 18.8 %fusion.21 = bf16[1,128,32]{1,2,0:T(8,128)(2,1)S(1)} fusion(f32[128,32]{0,1:T(8,128)S(1)} %fusion.27, f32[4096]{0:T(1024)S(1)} %bitcast.133, bf16[1,2,32,4096]{3,2,1,0:T(8,128)(2,1)S(1)} %copy-done.6), kind=kOutput, calls=%fused_computation.43 | convolution fusion | flops 42999808 | bytes 303104 | tf_op jit(solution)/shard_map/dot_general | solution.py:90
  46.6 20.8 %all-to-all-start = ((bf16[2,128,32]{2,0,1:T(2,128)(2,1)}), bf16[2,128,32]{2,0,1:T(2,128)(2,1)S(1)}, u32[]{:S(2)}, u32[]{:S(2)}) async-start(bf16[2,128,32]{2,0,1:T(2,128)(2,1)} %copy.73), calls=%async_computation | async-start | bytes 131072 | tf_op jit(solution)/shard_map/all_to_all | solution.py:152
  68.2 5.2 %select_add_fusion.1 = (f32[4,32,512]{2,1,0:T(8,128)S(1)}, f32[4,512,32]{1,2,0:T(8,128)S(1)}) fusion(f32[]{:T(128)} %bitcast.11, f32[]{:T(128)} %bitcast.10, f32[]{:T(128)} %bitcast.9, f32[]{:T(128)} %bitcast.8, f32[]{:T(128)} %bitcast.7, f32[]{:T(128)} %bitcast.6, f32[]{:T(128)} %bitcast.5, f32[]{:T(128)} %bitcast.4, s32[4,512]{1,0:T(4,128)S(1)} %bitcast.127), kind=kLoop, calls=%fused_computation.73 | loop fusion | flops 1572864 | bytes 532512 | tf_op jit(solution)/shard_map/add | solution.py:112
  73.4 6.6 %all-to-all-done = bf16[2,128,32]{2,0,1:T(2,128)(2,1)S(1)} async-done(((bf16[2,128,32]{2,0,1:T(2,128)(2,1)}), bf16[2,128,32]{2,0,1:T(2,128)(2,1)S(1)}, u32[]{:S(2)}, u32[]{:S(2)}) %all-to-all-start) | async-done | bytes 16416 | tf_op jit(solution)/shard_map/all_to_all | solution.py:152
  80.5 17.1 %fusion.25 = f32[128,128]{1,0:T(8,128)S(1)} fusion(f32[4096]{0:T(1024)S(1)} %reshape.365, f32[4096]{0:T(1024)S(1)} %reshape.364, s32[128]{0:T(128)S(1)} %iota_multiply_fusion, f32[4096]{0:T(1024)S(1)} %bitcast.134), kind=kOutput, calls=%fused_computation.47 | convolution fusion | flops 153616384 | bytes 115200 | tf_op jit(solution)/shard_map/dot_general | solution.py:90
  97.6 16.8 %fusion.24 = f32[128,128]{1,0:T(8,128)S(1)} fusion(f32[4096]{0:T(1024)S(1)} %reshape.365, f32[4096]{0:T(1024)S(1)} %reshape.364, s32[128]{0:T(128)S(1)} %iota_multiply_fusion, f32[4096]{0:T(1024)S(1)} %bitcast.135), kind=kOutput, calls=%fused_computation.46 | convolution fusion | flops 153092096 | bytes 115200 | tf_op jit(solution)/shard_map/dot_general | solution.py:90
  114.3 17.3 %fusion.16 = bf16[1,128,1,128]{3,1,2,0:T(8,128)(2,1)S(1)} fusion(f32[128,128]{1,0:T(8,128)S(1)} %fusion.25, f32[4096]{0:T(1024)S(1)} %reshape.365, f32[4096]{0:T(1024)S(1)} %reshape.364, s32[128]{0:T(128)S(1)} %iota_multiply_fusion, f32[4096]{0:T(1024)S(1)} %bitcast.136), kind=kOutput, calls=%fused_computation.36 | convolution fusion | flops 153124864 | bytes 147968 | tf_op jit(solution)/shard_map/dot_general | solution.py:90
  131.7 16.9 %fusion.17 = bf16[1,128,1,128]{3,1,2,0:T(8,128)(2,1)S(1)} fusion(f32[128,128]{1,0:T(8,128)S(1)} %fusion.24, f32[4096]{0:T(1024)S(1)} %reshape.365, f32[4096]{0:T(1024)S(1)} %reshape.364, s32[128]{0:T(128)S(1)} %iota_multiply_fusion, f32[4096]{0:T(1024)S(1)} %bitcast.137), kind=kOutput, calls=%fused_computation.37 | convolution fusion | flops 153649152 | bytes 147968 | tf_op jit(solution)/shard_map/dot_general | solution.py:90
  149.3 7.5 %all-to-all-start.1 = ((bf16[2,128,1,128]{3,0,2,1:T(2,128)(2,1)}), bf16[2,128,1,128]{3,0,2,1:T(2,128)(2,1)S(1)}, u32[]{:S(2)}, u32[]{:S(2)}) async-start(bf16[2,128,1,128]{3,0,2,1:T(2,128)(2,1)} %copy.74), calls=%async_computation.1 | async-start | bytes 131072 | tf_op jit(solution)/shard_map/all_to_all | solution.py:171
  156.8 11.5 %all-to-all-done.1 = bf16[2,128,1,128]{3,0,2,1:T(2,128)(2,1)S(1)} async-done(((bf16[2,128,1,128]{3,0,2,1:T(2,128)(2,1)}), bf16[2,128,1,128]{3,0,2,1:T(2,128)(2,1)S(1)}, u32[]{:S(2)}, u32[]{:S(2)}) %all-to-all-start.1) | async-done | bytes 65568 | tf_op jit(solution)/shard_map/all_to_all | solution.py:171
  168.9 3.9 %all-to-all-start.2 = ((bf16[4,2,32,1,1,128]{5,2,1,4,3,0:T(8,128)(2,1)}), bf16[4,2,32,1,1,128]{5,2,1,4,3,0:T(8,128)(2,1)S(1)}, u32[]{:S(2)}, u32[]{:S(2)}) async-start(bf16[4,2,32,1,1,128]{5,2,1,4,3,0:T(8,128)(2,1)} %broadcast_in_dim.12), calls=%async_computation.2 | async-start | bytes 131072 | tf_op jit(solution)/shard_map/all_to_all | solution.py:26
  172.8 4.5 %all-to-all-done.2 = bf16[4,2,32,1,1,128]{5,2,1,4,3,0:T(8,128)(2,1)S(1)} async-done(((bf16[4,2,32,1,1,128]{5,2,1,4,3,0:T(8,128)(2,1)}), bf16[4,2,32,1,1,128]{5,2,1,4,3,0:T(8,128)(2,1)S(1)}, u32[]{:S(2)}, u32[]{:S(2)}) %all-to-all-start.2) | async-done | bytes 65568 | tf_op jit(solution)/shard_map/all_to_all | solution.py:26
  177.5 2.4 collective-permute-start
  179.8 7.4 %collective-permute-start.1 = (bf16[2,128,32]{2,1,0:T(8,128)(2,1)S(1)}, bf16[2,128,32]{2,1,0:T(8,128)(2,1)S(1)}, u32[]{:S(2)}, u32[]{:S(2)}) collective-permute-start(bf16[2,128,32]{2,1,0:T(8,128)(2,1)S(1)} %get-tuple-element.39), channel_id=1, source_target_pairs={{4,0},{8,4},{12,8},{16,12},{20,16},{24,20},{28,24},{32,28},{36,32}... | collective-permute-start | bytes 49160 | tf_op jit(solution)/shard_map/ppermute | solution.py:42
  189.9 5.4 %fusion.13 = f32[4,512,2]{1,2,0:T(2,128)S(1)} fusion(f32[4,512,32]{1,2,0:T(8,128)S(1)} %get-tuple-element.41, s32[4,512]{1,0:T(4,128)S(1)} %bitcast.138, f32[]{:T(128)} %bitcast.11, f32[]{:T(128)} %bitcast.10, f32[]{:T(128)} %bitcast.9, f32[]{:T(128)} %bitcast.8, f32[]{:T(128)} %bitcast.7, f32[]{:T(128)} %bitcast.6, f32[]{:T(128)} %bitcast.5, f32[]{:T(128)} %bitcast.4, ...), kind=kOutput, calls=%fused_computation.30 | convolution fusion | flops 10227712 | bytes 303140 | tf_op jit(solution)/shard_map/cpab,pav->cpbv/dot_general | solution.py:124
  195.4 5.4 %convolution_bitcast_fusion.2 = bf16[2,4,32,32]{2,3,0,1:T(8,128)(2,1)S(1)} fusion(f32[4,32,512]{2,1,0:T(8,128)S(1)} %get-tuple-element.40, f32[2,4,512]{2,0,1:T(2,128)S(1)} %copy.80, s32[4,512]{1,0:T(4,128)S(1)} %bitcast.139, f32[]{:T(128)} %bitcast.11, f32[]{:T(128)} %bitcast.10, f32[]{:T(128)} %bitcast.9, f32[]{:T(128)} %bitcast.8, f32[]{:T(128)} %bitcast.7, ...), kind=kOutput, calls=%fused_computation.31 | convolution fusion | flops 10092544 | bytes 303136 | tf_op jit(solution)/shard_map/pav,cpbv->cpab/dot_general | solution.py:131
  202.1 1.9 collective-permute-start.2
  204.1 8.8 %collective-permute-start.3 = (bf16[2,128,32]{1,2,0:T(8,128)(2,1)S(1)}, bf16[2,128,32]{1,2,0:T(8,128)(2,1)S(1)}, u32[]{:S(2)}, u32[]{:S(2)}) collective-permute-start(bf16[2,128,32]{1,2,0:T(8,128)(2,1)S(1)} %get-tuple-element.36), channel_id=1, source_target_pairs={{4,0},{8,4},{12,8},{16,12},{20,16},{24,20},{28,24},{32,28},{36,32}... | collective-permute-start | bytes 49160 | tf_op jit(solution)/shard_map/ppermute | solution.py:56
  213.9 26.2 %all_to_all.28 = bf16[2,128,1,128]{3,0,2,1:T(2,128)(2,1)S(1)} all-to-all(bf16[2,128,1,128]{3,0,2,1:T(2,128)(2,1)S(1)} %copy.84), channel_id=1, replica_groups=mesh['role_0'=2,'role_1'=2,'grp'=32,'rep'=4] {'grp','rep'}, dimensions={1} | all-to-all | bytes 131072 | tf_op jit(solution)/shard_map/all_to_all | solution.py:187
  240.2 3.3 %all-gather = bf16[4,32,128]{2,1,0:T(8,128)(2,1)S(1)} all-gather(bf16[2,32,128]{2,1,0:T(8,128)(2,1)S(1)} %bitcast.125), channel_id=2, replica_groups=mesh['role_0'=2,'role_1'=2,'grp'=32,'rep'=4] {'role_0'}, dimensions={0}, use_global_device_ids=true | all-gather | bytes 49152 | tf_op jit(solution)/shard_map/all_gather | solution.py:62
  243.5 1.8 all_gather.7
  (64 shorter events, 9.3 us)
Async XLA Ops:
  0.6 9.9 %copy-start.6 = (bf16[1,2,32,4096]{3,2,1,0:T(8,128)(2,1)S(1)}, bf16[1,2,32,4096]{3,2,1,0:T(8,128)(2,1)}, u32[]{:S(2)}) copy-start(bf16[1,2,32,4096]{3,2,1,0:T(8,128)(2,1)} %param.12) | copy-start | bytes 1572868
  0.6 9.9 %copy-start.7 = (f32[1,4096]{1,0:T(1,128)S(1)}, f32[1,4096]{1,0:T(1,128)}, u32[]{:S(2)}) copy-start(f32[1,4096]{1,0:T(1,128)} %param.13) | copy-start | bytes 49156
  27.0 40.5 %copy-start.1 = (f32[8]{0:T(128)S(1)}, f32[8]{0:T(128)}, u32[]{:S(2)}) copy-start(f32[8]{0:T(128)} %param.14) | copy-start | bytes 100
  27.0 41.1 %copy-start.5 = (s32[1,4]{1,0:T(1,128)S(1)}, s32[1,4]{1,0:T(1,128)}, u32[]{:S(2)}) copy-start(s32[1,4]{1,0:T(1,128)} %param.17) | copy-start | bytes 52
  27.0 41.2 %copy-start.3 = (s32[1,4,512]{2,1,0:T(4,128)S(1)}, s32[1,4,512]{2,1,0:T(4,128)}, u32[]{:S(2)}) copy-start(s32[1,4,512]{2,1,0:T(4,128)} %param.19) | copy-start | bytes 24580
  46.6 33.3 %all-to-all-start = ((bf16[2,128,32]{2,0,1:T(2,128)(2,1)}), bf16[2,128,32]{2,0,1:T(2,128)(2,1)S(1)}, u32[]{:S(2)}, u32[]{:S(2)}) async-start(bf16[2,128,32]{2,0,1:T(2,128)(2,1)} %copy.73), calls=%async_computation | async-start | bytes 131072 | tf_op jit(solution)/shard_map/all_to_all | solution.py:152
  131.7 25.1 %copy-start.4 = (s32[1,4]{1,0:T(1,128)S(1)}, s32[1,4]{1,0:T(1,128)}, u32[]{:S(2)}) copy-start(s32[1,4]{1,0:T(1,128)} %param.16) | copy-start | bytes 52
  149.3 19.0 %all-to-all-start.1 = ((bf16[2,128,1,128]{3,0,2,1:T(2,128)(2,1)}), bf16[2,128,1,128]{3,0,2,1:T(2,128)(2,1)S(1)}, u32[]{:S(2)}, u32[]{:S(2)}) async-start(bf16[2,128,1,128]{3,0,2,1:T(2,128)(2,1)} %copy.74), calls=%async_computation.1 | async-start | bytes 131072 | tf_op jit(solution)/shard_map/all_to_all | solution.py:171
  168.9 8.4 %all-to-all-start.2 = ((bf16[4,2,32,1,1,128]{5,2,1,4,3,0:T(8,128)(2,1)}), bf16[4,2,32,1,1,128]{5,2,1,4,3,0:T(8,128)(2,1)S(1)}, u32[]{:S(2)}, u32[]{:S(2)}) async-start(bf16[4,2,32,1,1,128]{5,2,1,4,3,0:T(8,128)(2,1)} %broadcast_in_dim.12), calls=%async_computation.2 | async-start | bytes 131072 | tf_op jit(solution)/shard_map/all_to_all | solution.py:26
  177.5 10.0 %collective-permute-start = (bf16[2,128,32]{2,1,0:T(8,128)(2,1)S(1)}, bf16[2,128,32]{2,1,0:T(8,128)(2,1)S(1)}, u32[]{:S(2)}, u32[]{:S(2)}) collective-permute-start(bf16[2,128,32]{2,1,0:T(8,128)(2,1)S(1)} %get-tuple-element.38), channel_id=1, source_target_pairs={{0,4},{4,8},{8,12},{12,16},{16,20},{20,24},{24,28},{28,32},{32,36}... | collective-permute-start | bytes 49160 | tf_op jit(solution)/shard_map/ppermute | solution.py:41
  179.8 8.7 %collective-permute-start.1 = (bf16[2,128,32]{2,1,0:T(8,128)(2,1)S(1)}, bf16[2,128,32]{2,1,0:T(8,128)(2,1)S(1)}, u32[]{:S(2)}, u32[]{:S(2)}) collective-permute-start(bf16[2,128,32]{2,1,0:T(8,128)(2,1)S(1)} %get-tuple-element.39), channel_id=1, source_target_pairs={{4,0},{8,4},{12,8},{16,12},{20,16},{24,20},{28,24},{32,28},{36,32}... | collective-permute-start | bytes 49160 | tf_op jit(solution)/shard_map/ppermute | solution.py:42
  188.7 1.2 copy-start.8
  189.9 5.4 %copy-start.2 = (f32[2,1,4,512]{3,2,1,0:T(4,128)S(1)}, f32[2,1,4,512]{3,2,1,0:T(4,128)}, u32[]{:S(2)}) copy-start(f32[2,1,4,512]{3,2,1,0:T(4,128)} %param.15) | copy-start | bytes 49156
  195.3 5.4 %copy-start = (f32[2,4,512]{2,1,0:T(4,128)}, f32[2,4,512]{2,1,0:T(4,128)S(1)}, u32[]{:S(2)}) copy-start(f32[2,4,512]{2,1,0:T(4,128)S(1)} %fusion.71) | copy-start | bytes 49156
  202.1 10.8 %collective-permute-start.2 = (bf16[2,128,32]{1,2,0:T(8,128)(2,1)S(1)}, bf16[2,128,32]{1,2,0:T(8,128)(2,1)S(1)}, u32[]{:S(2)}, u32[]{:S(2)}) collective-permute-start(bf16[2,128,32]{1,2,0:T(8,128)(2,1)S(1)} %get-tuple-element.37), channel_id=1, source_target_pairs={{0,4},{4,8},{8,12},{12,16},{16,20},{20,24},{24,28},{28,32},{32,36}... | collective-permute-start | bytes 49160 | tf_op jit(solution)/shard_map/ppermute | solution.py:56
  204.1 9.7 %collective-permute-start.3 = (bf16[2,128,32]{1,2,0:T(8,128)(2,1)S(1)}, bf16[2,128,32]{1,2,0:T(8,128)(2,1)S(1)}, u32[]{:S(2)}, u32[]{:S(2)}) collective-permute-start(bf16[2,128,32]{1,2,0:T(8,128)(2,1)S(1)} %get-tuple-element.36), channel_id=1, source_target_pairs={{4,0},{8,4},{12,8},{16,12},{20,16},{24,20},{28,24},{32,28},{36,32}... | collective-permute-start | bytes 49160 | tf_op jit(solution)/shard_map/ppermute | solution.py:56
where the time goes:
time: 251 us; the launch traced here: 246 us
  matrix products  124 us (49%)
  starting transfers between devices  52.7 us (21%)
  blocking collectives  31.3 us (12%)
  waiting for transfers between devices  24.6 us (10%)
  local copies, waits for them, and re-layouts  6.05 us (2%)
  other arithmetic  5.94 us (2%)
    dot_general x8, matrix products, contract(): lax.dot_general(left, right, (((1,), (1,)), ((), ())), preferred_element_...  113 us
    all_to_all x1, blocking collectives, local(): lax.all_to_all(pieces.astype(jnp.bfloat16), ('grp', 'rep'), split_axis=1,...  26.2 us
    all_to_all x1, starting transfers between devices, local(): lax.all_to_all(partial_value, ('grp', 'rep'), split_axis=1, concat_axis=2...  20.8 us
    all_to_all x1, waiting for transfers between devices, local(): lax.all_to_all(contrib, ROLE_GRP, split_axis=1, concat_axis=2, tiled=True)  11.5 us
    ppermute x2, starting transfers between devices, shifted(): return lax.ppermute(value, axis, pairs)  10.8 us
    all_to_all x1, starting transfers between devices, local(): lax.all_to_all(contrib, ROLE_GRP, split_axis=1, concat_axis=2, tiled=True)  7.46 us
    ppermute x1, starting transfers between devices, extended(): lax.ppermute(leading, axis, [(b, a) for a, b in up])  7.43 us
    all_to_all x1, waiting for transfers between devices, local(): lax.all_to_all(partial_value, ('grp', 'rep'), split_axis=1, concat_axis=2...  6.6 us
  transfers between devices with their start and end apart: 7, of which 6 were waited for; matrix products, arithmetic and copies ran while one was open for 2% of the time, Pallas kernels for 0%

commit v1 on v0

v1 whole, which is shorter than its diff:
```python
import math

import jax
import jax.numpy as jnp
import numpy as np
from jax import lax
from jax.experimental import pallas as pl
from jax.experimental.pallas import tpu as pltpu
from jax.sharding import PartitionSpec as P

F = 4096
C = 128
PATCH = 32
KW = 8
NP_LOCAL = 4
KMAX = 512
ROLES = 4
GRPS = 32
REPS = 4
MESH = pl.DeviceIdType.MESH
bf16 = jnp.bfloat16
f32 = jnp.float32


def row_order():
    place = np.arange(C)
    return 4 * (place % GRPS) + place // GRPS


def tables():
    turn = 2.0 * math.pi
    row = row_order()
    cell = np.arange(128)
    block = np.arange(32)
    angle = turn * ((cell[:, None] * row[None, :]) % F) / F
    near = np.concatenate([np.cos(angle), -np.sin(angle)], axis=1)
    angle = turn * ((block[:, None] * row[None, :]) % 32) / 32
    far = np.concatenate([np.cos(angle), -np.sin(angle)], axis=1) / math.sqrt(F)
    angle = turn * ((cell[:, None] * block[None, :]) % 32) / 32
    cos, sin = np.cos(angle), np.sin(angle)
    first = np.block([[cos, sin], [-sin, cos]])
    angle = turn * ((cell[:, None] * cell[None, :]) % F) / F
    twist = np.concatenate([np.cos(angle), np.sin(angle)], axis=1)
    angle = turn * ((cell[:, None] * cell[None, :]) % 128) / 128
    cos, sin = np.cos(angle) / math.sqrt(F), np.sin(angle) / math.sqrt(F)
    second = np.concatenate([cos, sin, -sin, cos], axis=1)
    return (
        jnp.asarray(near, bf16),
        jnp.asarray(far, f32),
        jnp.asarray(first, bf16),
        jnp.asarray(twist, f32),
        jnp.asarray(second, bf16),
    )


def mm(left, right):
    return lax.dot_general(left, right, (((1,), (0,)), ((), ())), preferred_element_type=f32)


def mm_t(left, right):
    return lax.dot_general(left, right, (((1,), (1,)), ((), ())), preferred_element_type=f32)


def put_rows(ref, value):
    for i in range(value.shape[0]):
        ref[i, 0:1, :] = value[i : i + 1, :]


def get_rows(ref):
    return ref[...].reshape(ref.shape[0], ref.shape[2])


def body(
    facets, taper, taps, observed, patch_pos, counts, vis_u, vis_v,
    near, far, first, twist, second,
    residual, returned,
    x_out, x_in, q_out, q_in, u_out, u_in, s_out, s_in,
    y_out, y_in, z_out, z_in, f_out, f_in,
    ku, ku_low, kv, kv_wide, weights,
    sent, got,
):
    role, grp, rep = lax.axis_index("role"), lax.axis_index("grp"), lax.axis_index("rep")

    def near_peer(i):
        return (lax.rem(role + i // REPS, ROLES), grp, lax.rem(rep + i % REPS, REPS))

    def grp_peer(i):
        return lax.rem(grp + i, GRPS)

    barrier = pltpu.get_barrier_semaphore()

    def greet_near(i, _):
        pl.semaphore_signal(barrier, inc=1, device_id=near_peer(i), device_id_type=MESH)
        return 0

    def greet_grp(i, _):
        pl.semaphore_signal(barrier, inc=1, device_id=(role, grp_peer(i), rep), device_id_type=MESH)
        return 0

    lax.fori_loop(1, GRPS, greet_grp, 0)
    lax.fori_loop(1, ROLES * REPS, greet_near, 0)

    def push(src, dst, phase, device):
        pltpu.make_async_remote_copy(
            src_ref=src, dst_ref=dst, send_sem=sent.at[phase], recv_sem=got.at[phase],
            device_id=device, device_id_type=MESH,
        ).start()

    def keep(src, dst, phase):
        pltpu.make_async_copy(src, dst, got.at[phase]).start()

    def arrive(buffer, phase):
        pltpu.make_async_copy(buffer, buffer, got.at[phase]).wait()

    def drain(buffer, count, phase):
        part = buffer.at[pl.ds(0, count)]
        pltpu.make_async_copy(part, part, sent.at[phase]).wait()

    window = taper[...]
    data = [(facets[0, c].astype(f32) * window).astype(bf16) for c in range(2)]
    table = near[...]
    part_re = jnp.zeros((32, C), f32)
    part_im = jnp.zeros((32, C), f32)
    for chunk in range(4):
        blocks = []
        for i in range(8 * chunk, 8 * chunk + 8):
            blocks += [data[0][:, 128 * i : 128 * i + 128], data[1][:, 128 * i : 128 * i + 128]]
        spectrum = mm(jnp.concatenate(blocks, axis=0), table)
        for k in range(8):
            i = 8 * chunk + k
            of_re = spectrum[64 * k : 64 * k + 32]
            of_im = spectrum[64 * k + 32 : 64 * k + 64]
            t_re = of_re[:, :C] - of_im[:, C:]
            t_im = of_re[:, C:] + of_im[:, :C]
            e_re = far[i : i + 1, :C]
            e_im = far[i : i + 1, C:]
            part_re = part_re + (t_re * e_re - t_im * e_im)
            part_im = part_im + (t_re * e_im + t_im * e_re)
    turned = jnp.concatenate([part_re, part_im, part_re, part_im], axis=0).T
    lane = lax.broadcasted_iota(jnp.int32, (1, 128), 1)
    own = taper[:, pl.ds(pl.multiple_of(grp * 128, 128), 128)]
    mine = jnp.zeros((1, 128), f32)
    for r in range(REPS):
        moved = own if r == 0 else pltpu.roll(own, 128 - 32 * r, 1)
        mine = mine + moved * jnp.where(rep == r, 1.0, 0.0)
    mine = jnp.where(lane < 32, mine, 0.0)
    mine = mine + pltpu.roll(mine, 32, 1)
    mine = mine + pltpu.roll(mine, 64, 1)
    turned = turned * mine
    for r in range(REPS):
        low = turned[32 * r : 32 * r + 16]
        high = turned[32 * r + 16 : 32 * r + 32]
        x_out[r] = jnp.where(lane < 64, low, high).astype(bf16)

    pl.semaphore_wait(barrier, GRPS - 1 + ROLES * REPS - 1)

    slot = role * REPS + rep
    keep(x_out.at[rep], x_in.at[slot], 0)

    def send_near(i, _):
        device = near_peer(i)
        push(x_out.at[device[2]], x_in.at[slot], 0, device)
        return 0

    lax.fori_loop(1, ROLES * REPS, send_near, 0)
    arrive(x_in, 0)
    joined = [[jnp.zeros((16, 128), f32) for _ in range(2)] for _ in range(2)]
    for r in range(REPS):
        total = x_in[r].astype(f32)
        for k in range(1, ROLES):
            total = total + x_in[k * REPS + r].astype(f32)
        inside = (lane >= 32 * r) & (lane < 32 * r + 32)
        for h in range(2):
            for c in range(2):
                by = (32 * r - 64 * h - 32 * c) % 128
                moved = total if by == 0 else pltpu.roll(total, by, 1)
                joined[h][c] = jnp.where(inside, moved, joined[h][c])
    put_rows(q_out, jnp.concatenate([jnp.concatenate(joined[h], axis=1) for h in range(2)], axis=0))

    def swap(out, into, phase):
        keep(out.at[grp], into.at[grp], phase)

        def send(i, _):
            to = grp_peer(i)
            push(out.at[to], into.at[grp], phase, (role, to, rep))
            return 0

        lax.fori_loop(1, GRPS, send, 0)

    swap(q_out, q_in, 1)

    sub = role * GRPS + grp
    place = lax.broadcasted_iota(jnp.int32, (PATCH, KMAX), 0)
    row_in_patch = 4 * (place % 8) + place // 8
    has_left = jnp.where(sub > 0, 1, 0)
    has_right = jnp.where(sub < ROLES * GRPS - 1, 1, 0)

    def block_of(p):
        position = jnp.full((1, KMAX), patch_pos[0, p], jnp.int32)
        row_block = (
            jnp.where(position >= 6, 1, 0)
            + jnp.where(position >= 12, 1, 0)
            + jnp.where(position >= 18, 1, 0)
        )
        return row_block, position - 6 * row_block

    for p in range(NP_LOCAL):
        cols = slice(KMAX * p, KMAX * p + KMAX)
        row_block, col_block = block_of(p)
        du = row_in_patch - vis_u[0, p : p + 1, :]
        dv = place - vis_v[0, p : p + 1, :]
        u32 = jnp.zeros((PATCH, KMAX), f32)
        v32 = jnp.zeros((PATCH, KMAX), f32)
        for t in range(KW):
            u32 = jnp.where(du == t, taps[t], u32)
            v32 = jnp.where(dv == t, taps[t], v32)
        kv[:, cols] = v32
        for r in range(REPS):
            rows = u32[8 * r : 8 * r + 8]
            for h in range(2):
                pair = jnp.concatenate(
                    [jnp.where(row_block == 2 * h + k, rows, 0.0) for k in range(2)], axis=0
                )
                at = slice(32 * r + 16 * h, 32 * r + 16 * h + 16)
                ku[at, cols] = pair
                ku_low[at, cols] = pair.astype(bf16)
        for u in range(4):
            chosen = jnp.where(col_block == u + 1, 1, 0)
            if u == 2:
                chosen = chosen + jnp.where(col_block == 0, 1, 0) * has_left
            if u == 1:
                chosen = chosen + jnp.where(col_block == 5, 1, 0) * has_right
            kv_wide[32 * u : 32 * u + 32, cols] = jnp.where(chosen > 0, v32, 0.0).astype(bf16)

    arrive(q_in, 1)
    cells = get_rows(q_in)
    stacked = jnp.concatenate([cells[:, :128], cells[:, 128:]], axis=0).astype(bf16)
    mixed = mm(first[...], stacked)
    mixed_re, mixed_im = mixed[:128], mixed[128:]
    cos, sin = twist[:, :128], twist[:, 128:]
    both = jnp.concatenate(
        [mixed_re * cos + mixed_im * sin, mixed_im * cos - mixed_re * sin], axis=1
    ).astype(bf16)
    wave = second[pl.ds(pl.multiple_of(role * GRPS, GRPS), GRPS), :]
    put_rows(
        u_out, jnp.concatenate([mm_t(wave[:, :256], both), mm_t(wave[:, 256:], both)], axis=1)
    )
    swap(u_out, u_in, 2)
    arrive(u_in, 2)

    s_out[0] = get_rows(u_in).astype(bf16)
    keep(s_out.at[0], s_in.at[rep], 3)

    def send_rows(i, _):
        push(s_out.at[0], s_in.at[rep], 3, (role, grp, lax.rem(rep + i, REPS)))
        return 0

    lax.fori_loop(1, REPS, send_rows, 0)
    arrive(s_in, 3)

    rows = [s_in[r] for r in range(REPS)]
    grid_cells = jnp.concatenate(
        [row[:, :128] for row in rows] + [row[:, 128:] for row in rows], axis=0
    )
    slots = lax.broadcasted_iota(jnp.int32, (1, KMAX), 1)
    for p in range(NP_LOCAL):
        cols = slice(KMAX * p, KMAX * p + KMAX)
        _, col_block = block_of(p)
        live = slots < jnp.full((1, KMAX), counts[0, p], jnp.int32)
        along = mm(grid_cells, kv_wide[:, cols])
        ku_p = ku[:, cols]
        kv_p = kv[:, cols]
        for c in range(2):
            predicted = jnp.sum(along[128 * c : 128 * c + 128] * ku_p, axis=0, keepdims=True)
            left_over = jnp.where(live, observed[c, 0, p : p + 1, :] - predicted, 0.0)
            residual[c, 0, p : p + 1, :] = left_over
            weighted = kv_p * left_over
            for u in range(4):
                at = slice(128 * c + 32 * u, 128 * c + 32 * u + 32)
                weights[at, cols] = jnp.where(col_block == u + 1, weighted, 0.0).astype(bf16)
            at = slice(256 + 64 * c, 256 + 64 * c + 32)
            weights[at, cols] = jnp.where(col_block == 0, weighted, 0.0).astype(bf16)
            at = slice(288 + 64 * c, 288 + 64 * c + 32)
            weights[at, cols] = jnp.where(col_block == 5, weighted, 0.0).astype(bf16)
    gridded = mm_t(ku_low[...], weights[...])
    for r in range(REPS):
        y_out[r] = gridded[32 * r : 32 * r + 32].astype(bf16)

    keep(y_out.at[rep], y_in.at[rep], 4)

    def send_gridded(i, _):
        to = lax.rem(rep + i, REPS)
        push(y_out.at[to], y_in.at[rep], 4, (role, grp, to))
        return 0

    lax.fori_loop(1, REPS, send_gridded, 0)
    arrive(y_in, 4)
    total = y_in[0].astype(f32)
    for r in range(1, REPS):
        total = total + y_in[r].astype(f32)
    put_rows(z_out, total)
    swap(z_out, z_in, 5)
    arrive(z_in, 5)
    f_out[0] = get_rows(z_in).astype(bf16)
    keep(f_out.at[0], f_in.at[role], 6)

    def send_owned(i, _):
        push(f_out.at[0], f_in.at[role], 6, (lax.rem(role + i, ROLES), grp, rep))
        return 0

    lax.fori_loop(1, ROLES, send_owned, 0)
    arrive(f_in, 6)

    owned = jnp.concatenate([f_in[k] for k in range(ROLES)], axis=0).astype(f32)
    edges = owned[:, 256:]
    column = lax.broadcasted_iota(jnp.int32, (C, 128), 1)
    subgrid = lax.broadcasted_iota(jnp.int32, (C, 128), 0)
    for c in range(2):
        side = pltpu.roll(edges, 96 if c == 0 else 32, 1)
        from_left = jnp.where((column < 32) & (subgrid > 0), pltpu.roll(side, 1, 0), 0.0)
        from_right = jnp.where((column >= 96) & (subgrid < C - 1), pltpu.roll(side, C - 1, 0), 0.0)
        returned[c] = (owned[:, 128 * c : 128 * c + 128] + from_left + from_right).astype(bf16)

    drain(x_in, 15, 0)
    drain(q_in, 31, 1)
    drain(u_in, 31, 2)
    drain(s_in, 3, 3)
    drain(y_in, 3, 4)
    drain(z_in, 31, 5)
    drain(f_in, 3, 6)


def local(facets, taper, kernel, observed, patch_pos, counts, vis_u, vis_v):
    vmem = pl.BlockSpec(memory_space=pltpu.VMEM)
    smem = pl.BlockSpec(memory_space=pltpu.SMEM)
    residual, returned = pl.pallas_call(
        body,
        out_shape=(
            jax.ShapeDtypeStruct((2, 1, NP_LOCAL, KMAX), f32),
            jax.ShapeDtypeStruct((2, C, C), bf16),
        ),
        in_specs=[vmem, vmem, smem, vmem, smem, smem, vmem, vmem] + [vmem] * 5,
        out_specs=(vmem, vmem),
        scratch_shapes=[
            pltpu.VMEM((REPS, 16, 128), bf16),
            pltpu.VMEM((ROLES * REPS, 16, 128), bf16),
            pltpu.VMEM((GRPS, 1, 256), f32),
            pltpu.VMEM((GRPS, 1, 256), f32),
            pltpu.VMEM((GRPS, 1, 256), f32),
            pltpu.VMEM((GRPS, 1, 256), f32),
            pltpu.VMEM((1, 32, 256), bf16),
            pltpu.VMEM((REPS, 32, 256), bf16),
            pltpu.VMEM((REPS, 32, 384), bf16),
            pltpu.VMEM((REPS, 32, 384), bf16),
            pltpu.VMEM((GRPS, 1, 384), f32),
            pltpu.VMEM((GRPS, 1, 384), f32),
            pltpu.VMEM((1, 32, 384), bf16),
            pltpu.VMEM((ROLES, 32, 384), bf16),
            pltpu.VMEM((C, NP_LOCAL * KMAX), f32),
            pltpu.VMEM((C, NP_LOCAL * KMAX), bf16),
            pltpu.VMEM((PATCH, NP_LOCAL * KMAX), f32),
            pltpu.VMEM((C, NP_LOCAL * KMAX), bf16),
            pltpu.VMEM((384, NP_LOCAL * KMAX), bf16),
            pltpu.SemaphoreType.DMA((7,)),
            pltpu.SemaphoreType.DMA((7,)),
        ],
        compiler_params=pltpu.CompilerParams(collective_id=0, has_side_effects=True),
        name="cycle",
    )(facets, taper, kernel, observed, patch_pos, counts, vis_u, vis_v, *tables())
    return residual, returned.reshape(2, C, 1, C)


def solution(mesh):
    both = ("role", "grp")
    return jax.shard_map(
        local,
        mesh=mesh,
        in_specs=(
            P("role", None, ("grp", "rep"), None),
            P("role", None),
            P(),
            P(None, both, "rep", None),
            P(both, "rep"),
            P(both, "rep"),
            P(both, "rep", None),
            P(both, "rep", None),
        ),
        out_specs=(P(None, both, "rep", None), P(None, None, ("grp", "rep"), None)),
        check_vma=False,
    )
```

time: 251 us -> 58.3 us (0.23); the launches traced: 246 us -> 58 us
  matrix products: 124 us -> 0 us
  Pallas kernels: 0 us -> 54.6 us
  starting transfers between devices: 52.7 us -> 0 us
  blocking collectives: 31.3 us -> 0 us
  waiting for transfers between devices: 24.6 us -> 0 us
  other arithmetic: 5.94 us -> 0 us
  local copies, waits for them, and re-layouts: 6.05 us -> 2.8 us
    dot_general x11 -> x0, matrix products: 124 us -> none  [the longest x8 113 us: contract(): lax.dot_general(left, right, (((1,), (1,)), ((), ())), preferred_element_...]
    pallas_call x0 -> x1, Pallas kernels: none -> 54.6 us  [local(): pl.pallas_call(body, out_shape=(jax.ShapeDtypeStruct((2, 1, NP_LOCAL, KMA...]
    all_to_all x3 -> x0, starting transfers between devices: 32.1 us -> none  [the longest x1 20.8 us: local(): lax.all_to_all(partial_value, ('grp', 'rep'), split_axis=1, concat_axis=2...]
    all_to_all x1 -> x0, blocking collectives: 26.2 us -> none  [local(): lax.all_to_all(pieces.astype(jnp.bfloat16), ('grp', 'rep'), split_axis=1,...]
    all_to_all x3 -> x0, waiting for transfers between devices: 22.5 us -> none  [the longest x1 11.5 us: local(): lax.all_to_all(contrib, ROLE_GRP, split_axis=1, concat_axis=2, tiled=True)]
    ppermute x4 -> x0, starting transfers between devices: 20.5 us -> none  [the longest x2 10.8 us: shifted(): return lax.ppermute(value, axis, pairs)]
    add x1 -> x0, other arithmetic: 5.16 us -> none  [kernel_rows(): result + kernel[position] * (distance == position).astype(jnp.float32)]
    all_gather x2 -> x0, blocking collectives: 5.09 us -> none  [gather_in_order(): blocks = lax.all_gather(blocks, axes[k], axis=0, tiled=True)]
  transfers between devices with their start and end apart: 7 -> 0, of which waited for: 6 -> 0; matrix products, arithmetic and copies ran while one was open for 2% -> 0% of each run, Pallas kernels for 0% -> 0%
where the time goes in v1:
time: 58.3 us; the launch traced here: 58 us
  Pallas kernels  54.6 us (94%)
  local copies, waits for them, and re-layouts  2.8 us (5%)
  between operations  0.64 us (1%)
    pallas_call x1, Pallas kernels, local(): pl.pallas_call(body, out_shape=(jax.ShapeDtypeStruct((2, 1, NP_LOCAL, KMA...  54.6 us
    unnamed x2, local copies, waits for them, and re-layouts  2.8 us

profile of v1, /device:TPU:1, one launch (start us, length us, event | category | flops | bytes accessed | tf_op | source)
XLA Modules:
  0.0 58.0 jit_solution(5990024897407120118)
XLA Ops:
  0.6 54.6 %cycle.1 = (f32[2,1,4,512]{3,2,1,0:T(4,128)}, bf16[2,128,128]{2,1,0:T(8,128)(2,1)}) custom-call(bf16[1,2,32,4096]{3,2,1,0:T(8,128)(2,1)} %facets.1, f32[1,4096]{1,0:T(1,128)} %taper.1, f32[8]{0:T(128)} %taps.1, f32[2,1,4,512]{3,2,1,0:T(4,128)} %observed.1, s32[1,4]{1,0:T(1,128)} %patch_pos.1, s32[1,4]{1,0:T(1,128)} %counts.1, s32[1,4,512]{2,1,0:T(4,128)} %vis_u.1, ...), custom_call_target="tpu_custom_call" | custom-call | tf_op jit(solution)/shard_map/cycle/pallas_call | solution.py:336
  55.2 1.3 %copy.18 = f32[2,1,4,512]{3,2,1,0:T(4,128)} copy(f32[2,1,4,512]{3,2,1,0:T(4,128)} %get-tuple-element.10) | data formatting | bytes 32768
  56.6 1.5 %copy.19 = bf16[2,128,1,128]{3,1,2,0:T(8,128)(2,1)} copy(bf16[2,128,1,128]{3,1,2,0:T(8,128)(2,1)} %bitcast.3) | data formatting | bytes 131072

commit v2 on v1

--- a/solution.py
+++ b/solution.py
@@ -17,6 +17,8 @@
 ROLES = 4
 GRPS = 32
 REPS = 4
+NEAR = ROLES * REPS
+FAR = 13
 MESH = pl.DeviceIdType.MESH
 bf16 = jnp.bfloat16
 f32 = jnp.float32
@@ -43,7 +45,8 @@
     twist = np.concatenate([np.cos(angle), np.sin(angle)], axis=1)
     angle = turn * ((cell[:, None] * cell[None, :]) % 128) / 128
     cos, sin = np.cos(angle) / math.sqrt(F), np.sin(angle) / math.sqrt(F)
-    second = np.concatenate([cos, sin, -sin, cos], axis=1)
+    second = np.stack([np.concatenate([cos, sin], 1), np.concatenate([-sin, cos], 1)], axis=1)
+    second = second.reshape(ROLES, GRPS, 2, 256).transpose(1, 0, 2, 3).reshape(GRPS, 8, 256)
     return (
         jnp.asarray(near, bf16),
         jnp.asarray(far, f32),
@@ -71,13 +74,15 @@
 
 
 def body(
-    facets, taper, taps, observed, patch_pos, counts, vis_u, vis_v,
-    near, far, first, twist, second,
+    facets_far, taper_far, near_far, far_far, first_far, twist_far, second_far,
+    taps_far, observed_far, patch_pos_far, counts_far, vis_u_far, vis_v_far,
     residual, returned,
-    x_out, x_in, q_out, q_in, u_out, u_in, s_out, s_in,
+    facets, taper, near, far, first, twist, second,
+    taps, observed, patch_pos, counts, vis_u, vis_v,
+    x_out, x_in, q_out, q_in, q_all, u_all, u_out, s_in,
     y_out, y_in, z_out, z_in, f_out, f_in,
     ku, ku_low, kv, kv_wide, weights,
-    sent, got,
+    sent, got, loaded,
 ):
     role, grp, rep = lax.axis_index("role"), lax.axis_index("grp"), lax.axis_index("rep")
 
@@ -87,6 +92,22 @@
     def grp_peer(i):
         return lax.rem(grp + i, GRPS)
 
+    inputs = [
+        (taper_far, taper), (near_far, near), (far_far, far),
+        (first_far, first), (twist_far, twist), (second_far, second),
+        (taps_far, taps), (observed_far, observed), (patch_pos_far, patch_pos),
+        (counts_far, counts), (vis_u_far, vis_u), (vis_v_far, vis_v),
+    ]
+    loads = []
+    for k in range(4):
+        part = pl.ds(1024 * k, 1024)
+        loads.append((facets_far.at[0, :, :, part], facets.at[:, :, part]))
+    loads = [
+        pltpu.make_async_copy(src, dst, loaded.at[k]) for k, (src, dst) in enumerate(loads + inputs)
+    ]
+    for load in loads[4:7] + loads[:4] + loads[7:]:
+        load.start()
+
     barrier = pltpu.get_barrier_semaphore()
 
     def greet_near(i, _):
@@ -98,7 +119,7 @@
         return 0
 
     lax.fori_loop(1, GRPS, greet_grp, 0)
-    lax.fori_loop(1, ROLES * REPS, greet_near, 0)
+    lax.fori_loop(1, NEAR, greet_near, 0)
 
     def push(src, dst, phase, device):
         pltpu.make_async_remote_copy(
@@ -116,15 +137,17 @@
         part = buffer.at[pl.ds(0, count)]
         pltpu.make_async_copy(part, part, sent.at[phase]).wait()
 
-    window = taper[...]
-    data = [(facets[0, c].astype(f32) * window).astype(bf16) for c in range(2)]
+    for load in loads[4:7]:
+        load.wait()
     table = near[...]
     part_re = jnp.zeros((32, C), f32)
     part_im = jnp.zeros((32, C), f32)
     for chunk in range(4):
+        loads[chunk].wait()
         blocks = []
         for i in range(8 * chunk, 8 * chunk + 8):
-            blocks += [data[0][:, 128 * i : 128 * i + 128], data[1][:, 128 * i : 128 * i + 128]]
+            at = slice(128 * i, 128 * i + 128)
+            blocks += [(facets[c, :, at].astype(f32) * taper[:, at]).astype(bf16) for c in range(2)]
         spectrum = mm(jnp.concatenate(blocks, axis=0), table)
         for k in range(8):
             i = 8 * chunk + k
@@ -147,48 +170,47 @@
     mine = mine + pltpu.roll(mine, 32, 1)
     mine = mine + pltpu.roll(mine, 64, 1)
     turned = turned * mine
-    for r in range(REPS):
-        low = turned[32 * r : 32 * r + 16]
-        high = turned[32 * r + 16 : 32 * r + 32]
-        x_out[r] = jnp.where(lane < 64, low, high).astype(bf16)
-
-    pl.semaphore_wait(barrier, GRPS - 1 + ROLES * REPS - 1)
+    for k in range(NEAR):
+        x_out[k] = turned[8 * k : 8 * k + 8].astype(bf16)
+
+    pl.semaphore_wait(barrier, GRPS + NEAR - 2)
 
     slot = role * REPS + rep
-    keep(x_out.at[rep], x_in.at[slot], 0)
-
-    def send_near(i, _):
-        device = near_peer(i)
-        push(x_out.at[device[2]], x_in.at[slot], 0, device)
-        return 0
-
-    lax.fori_loop(1, ROLES * REPS, send_near, 0)
+
+    def spread(out, into, phase):
+        keep(out.at[slot], into.at[slot], phase)
+
+        def send(i, _):
+            device = near_peer(i)
+            push(out.at[device[0] * REPS + device[2]], into.at[slot], phase, device)
+            return 0
+
+        lax.fori_loop(1, NEAR, send, 0)
+
+    spread(x_out, x_in, 0)
     arrive(x_in, 0)
-    joined = [[jnp.zeros((16, 128), f32) for _ in range(2)] for _ in range(2)]
+    cell_re = jnp.zeros((8, 128), f32)
+    cell_im = jnp.zeros((8, 128), f32)
     for r in range(REPS):
         total = x_in[r].astype(f32)
         for k in range(1, ROLES):
             total = total + x_in[k * REPS + r].astype(f32)
         inside = (lane >= 32 * r) & (lane < 32 * r + 32)
-        for h in range(2):
-            for c in range(2):
-                by = (32 * r - 64 * h - 32 * c) % 128
-                moved = total if by == 0 else pltpu.roll(total, by, 1)
-                joined[h][c] = jnp.where(inside, moved, joined[h][c])
-    put_rows(q_out, jnp.concatenate([jnp.concatenate(joined[h], axis=1) for h in range(2)], axis=0))
-
-    def swap(out, into, phase):
-        keep(out.at[grp], into.at[grp], phase)
-
-        def send(i, _):
-            to = grp_peer(i)
-            push(out.at[to], into.at[grp], phase, (role, to, rep))
-            return 0
-
-        lax.fori_loop(1, GRPS, send, 0)
-
-    swap(q_out, q_in, 1)
-
+        moved = pltpu.roll(total, 32, 1)
+        cell_re = jnp.where(inside, total if r % 2 == 0 else moved, cell_re)
+        cell_im = jnp.where(inside, moved if r % 2 == 0 else total, cell_im)
+    q_out[0] = jnp.concatenate([cell_re, cell_im], axis=1).astype(bf16)
+    keep(q_out.at[0], q_in.at[grp], 1)
+
+    def send_cells(i, _):
+        push(q_out.at[0], q_in.at[grp], 1, (role, grp_peer(i), rep))
+        return 0
+
+    lax.fori_loop(FAR, GRPS, send_cells, 0)
+    lax.fori_loop(1, FAR, send_cells, 0)
+
+    for load in loads[7:]:
+        load.wait()
     sub = role * GRPS + grp
     place = lax.broadcasted_iota(jnp.int32, (PATCH, KMAX), 0)
     row_in_patch = 4 * (place % 8) + place // 8
@@ -196,7 +218,7 @@
     has_right = jnp.where(sub < ROLES * GRPS - 1, 1, 0)
 
     def block_of(p):
-        position = jnp.full((1, KMAX), patch_pos[0, p], jnp.int32)
+        position = jnp.broadcast_to(patch_pos[0:1, p : p + 1], (1, KMAX))
         row_block = (
             jnp.where(position >= 6, 1, 0)
             + jnp.where(position >= 12, 1, 0)
@@ -204,6 +226,7 @@
         )
         return row_block, position - 6 * row_block
 
+    tap = [jnp.broadcast_to(taps[0:1, t : t + 1], (PATCH, KMAX)) for t in range(KW)]
     for p in range(NP_LOCAL):
         cols = slice(KMAX * p, KMAX * p + KMAX)
         row_block, col_block = block_of(p)
@@ -212,8 +235,8 @@
         u32 = jnp.zeros((PATCH, KMAX), f32)
         v32 = jnp.zeros((PATCH, KMAX), f32)
         for t in range(KW):
-            u32 = jnp.where(du == t, taps[t], u32)
-            v32 = jnp.where(dv == t, taps[t], v32)
+            u32 = jnp.where(du == t, tap[t], u32)
+            v32 = jnp.where(dv == t, tap[t], v32)
         kv[:, cols] = v32
         for r in range(REPS):
             rows = u32[8 * r : 8 * r + 8]
@@ -233,40 +256,45 @@
             kv_wide[32 * u : 32 * u + 32, cols] = jnp.where(chosen > 0, v32, 0.0).astype(bf16)
 
     arrive(q_in, 1)
-    cells = get_rows(q_in)
-    stacked = jnp.concatenate([cells[:, :128], cells[:, 128:]], axis=0).astype(bf16)
-    mixed = mm(first[...], stacked)
-    mixed_re, mixed_im = mixed[:128], mixed[128:]
+    for k in range(GRPS):
+        arrived = q_in[k].astype(f32)
+        q_all[8 * k : 8 * k + 8, :] = arrived[:, :128]
+        q_all[8 * GRPS + 8 * k : 8 * GRPS + 8 * k + 8, :] = arrived[:, 128:]
+    stacked = []
+    for k in range(8):
+        stacked.append(q_all[pl.ds(k, 2 * GRPS, stride=8), :].astype(bf16))
+    mixed = mm(first[...], jnp.concatenate(stacked, axis=1))
     cos, sin = twist[:, :128], twist[:, 128:]
-    both = jnp.concatenate(
-        [mixed_re * cos + mixed_im * sin, mixed_im * cos - mixed_re * sin], axis=1
-    ).astype(bf16)
-    wave = second[pl.ds(pl.multiple_of(role * GRPS, GRPS), GRPS), :]
-    put_rows(
-        u_out, jnp.concatenate([mm_t(wave[:, :256], both), mm_t(wave[:, 256:], both)], axis=1)
-    )
-    swap(u_out, u_in, 2)
-    arrive(u_in, 2)
-
-    s_out[0] = get_rows(u_in).astype(bf16)
-    keep(s_out.at[0], s_in.at[rep], 3)
+    both = []
+    for k in range(8):
+        mixed_re = mixed[:128, 128 * k : 128 * k + 128]
+        mixed_im = mixed[128:, 128 * k : 128 * k + 128]
+        pair = [mixed_re * cos + mixed_im * sin, mixed_im * cos - mixed_re * sin]
+        both.append(jnp.concatenate(pair, axis=1).astype(bf16))
+    waves = mm_t(second[grp], jnp.concatenate(both, axis=0))
+    for k in range(8):
+        u_all[8 * k : 8 * k + 8, :] = waves[:, 128 * k : 128 * k + 128]
+    for k in range(ROLES):
+        pair = [u_all[pl.ds(2 * k + c, 8, stride=8), :] for c in range(2)]
+        u_out[k] = jnp.concatenate(pair, axis=1).astype(bf16)
+
+    keep(u_out.at[role], s_in.at[slot], 2)
 
     def send_rows(i, _):
-        push(s_out.at[0], s_in.at[rep], 3, (role, grp, lax.rem(rep + i, REPS)))
-        return 0
-
-    lax.fori_loop(1, REPS, send_rows, 0)
-    arrive(s_in, 3)
-
-    rows = [s_in[r] for r in range(REPS)]
-    grid_cells = jnp.concatenate(
-        [row[:, :128] for row in rows] + [row[:, 128:] for row in rows], axis=0
-    )
+        device = near_peer(i)
+        push(u_out.at[device[0]], s_in.at[slot], 2, device)
+        return 0
+
+    lax.fori_loop(1, NEAR, send_rows, 0)
+    arrive(s_in, 2)
+
+    rows = jnp.concatenate([s_in[k].astype(f32) for k in range(NEAR)], axis=0).astype(bf16)
+    grid_cells = jnp.concatenate([rows[:, :128], rows[:, 128:]], axis=0)
     slots = lax.broadcasted_iota(jnp.int32, (1, KMAX), 1)
     for p in range(NP_LOCAL):
         cols = slice(KMAX * p, KMAX * p + KMAX)
         _, col_block = block_of(p)
-        live = slots < jnp.full((1, KMAX), counts[0, p], jnp.int32)
+        live = slots < jnp.broadcast_to(counts[0:1, p : p + 1], (1, KMAX))
         along = mm(grid_cells, kv_wide[:, cols])
         ku_p = ku[:, cols]
         kv_p = kv[:, cols]
@@ -286,30 +314,38 @@
     for r in range(REPS):
         y_out[r] = gridded[32 * r : 32 * r + 32].astype(bf16)
 
-    keep(y_out.at[rep], y_in.at[rep], 4)
+    keep(y_out.at[rep], y_in.at[rep], 3)
 
     def send_gridded(i, _):
         to = lax.rem(rep + i, REPS)
-        push(y_out.at[to], y_in.at[rep], 4, (role, grp, to))
+        push(y_out.at[to], y_in.at[rep], 3, (role, grp, to))
         return 0
 
     lax.fori_loop(1, REPS, send_gridded, 0)
-    arrive(y_in, 4)
+    arrive(y_in, 3)
     total = y_in[0].astype(f32)
     for r in range(1, REPS):
         total = total + y_in[r].astype(f32)
     put_rows(z_out, total)
-    swap(z_out, z_in, 5)
-    arrive(z_in, 5)
+    keep(z_out.at[grp], z_in.at[grp], 4)
+
+    def send_owner(i, _):
+        to = grp_peer(i)
+        push(z_out.at[to], z_in.at[grp], 4, (role, to, rep))
+        return 0
+
+    lax.fori_loop(FAR, GRPS, send_owner, 0)
+    lax.fori_loop(1, FAR, send_owner, 0)
+    arrive(z_in, 4)
     f_out[0] = get_rows(z_in).astype(bf16)
-    keep(f_out.at[0], f_in.at[role], 6)
+    keep(f_out.at[0], f_in.at[role], 5)
 
     def send_owned(i, _):
-        push(f_out.at[0], f_in.at[role], 6, (lax.rem(role + i, ROLES), grp, rep))
+        push(f_out.at[0], f_in.at[role], 5, (lax.rem(role + i, ROLES), grp, rep))
         return 0
 
     lax.fori_loop(1, ROLES, send_owned, 0)
-    arrive(f_in, 6)
+    arrive(f_in, 5)
 
     owned = jnp.concatenate([f_in[k] for k in range(ROLES)], axis=0).astype(f32)
     edges = owned[:, 256:]
@@ -321,35 +357,47 @@
         from_right = jnp.where((column >= 96) & (subgrid < C - 1), pltpu.roll(side, C - 1, 0), 0.0)
         returned[c] = (owned[:, 128 * c : 128 * c + 128] + from_left + from_right).astype(bf16)
 
-    drain(x_in, 15, 0)
-    drain(q_in, 31, 1)
-    drain(u_in, 31, 2)
-    drain(s_in, 3, 3)
-    drain(y_in, 3, 4)
-    drain(z_in, 31, 5)
-    drain(f_in, 3, 6)
+    drain(x_in, NEAR - 1, 0)
+    drain(q_in, GRPS - 1, 1)
+    drain(s_in, NEAR - 1, 2)
+    drain(y_in, REPS - 1, 3)
+    drain(z_in, GRPS - 1, 4)
+    drain(f_in, ROLES - 1, 5)
 
 
 def local(facets, taper, kernel, observed, patch_pos, counts, vis_u, vis_v):
     vmem = pl.BlockSpec(memory_space=pltpu.VMEM)
-    smem = pl.BlockSpec(memory_space=pltpu.SMEM)
+    hbm = pl.BlockSpec(memory_space=pltpu.HBM)
     residual, returned = pl.pallas_call(
         body,
         out_shape=(
-            jax.ShapeDtypeStruct((2, 1, NP_LOCAL, KMAX), f32),
-            jax.ShapeDtypeStruct((2, C, C), bf16),
+            pltpu.VMEM((2, 1, NP_LOCAL, KMAX), f32),
+            pltpu.VMEM((2, C, C), bf16),
         ),
-        in_specs=[vmem, vmem, smem, vmem, smem, smem, vmem, vmem] + [vmem] * 5,
+        in_specs=[hbm] * 13,
         out_specs=(vmem, vmem),
         scratch_shapes=[
-            pltpu.VMEM((REPS, 16, 128), bf16),
-            pltpu.VMEM((ROLES * REPS, 16, 128), bf16),
-            pltpu.VMEM((GRPS, 1, 256), f32),
-            pltpu.VMEM((GRPS, 1, 256), f32),
-            pltpu.VMEM((GRPS, 1, 256), f32),
-            pltpu.VMEM((GRPS, 1, 256), f32),
-            pltpu.VMEM((1, 32, 256), bf16),
-            pltpu.VMEM((REPS, 32, 256), bf16),
+            pltpu.VMEM((2, 32, F), bf16),
+            pltpu.VMEM((1, F), f32),
+            pltpu.VMEM((128, 256), bf16),
+            pltpu.VMEM((32, 256), f32),
+            pltpu.VMEM((256, 64), bf16),
+            pltpu.VMEM((128, 256), f32),
+            pltpu.VMEM((GRPS, 8, 256), bf16),
+            pltpu.VMEM((1, KW), f32),
+            pltpu.VMEM((2, 1, NP_LOCAL, KMAX), f32),
+            pltpu.VMEM((1, NP_LOCAL), jnp.int32),
+            pltpu.VMEM((1, NP_LOCAL), jnp.int32),
+            pltpu.VMEM((1, NP_LOCAL, KMAX), jnp.int32),
+            pltpu.VMEM((1, NP_LOCAL, KMAX), jnp.int32),
+            pltpu.VMEM((NEAR, 8, 128), bf16),
+            pltpu.VMEM((NEAR, 8, 128), bf16),
+            pltpu.VMEM((1, 8, 256), bf16),
+            pltpu.VMEM((GRPS, 8, 256), bf16),
+            pltpu.VMEM((16 * GRPS, 128), f32),
+            pltpu.VMEM((64, 128), f32),
+            pltpu.VMEM((ROLES, 8, 256), bf16),
+            pltpu.VMEM((NEAR, 8, 256), bf16),
             pltpu.VMEM((REPS, 32, 384), bf16),
             pltpu.VMEM((REPS, 32, 384), bf16),
             pltpu.VMEM((GRPS, 1, 384), f32),
@@ -361,12 +409,15 @@
             pltpu.VMEM((PATCH, NP_LOCAL * KMAX), f32),
             pltpu.VMEM((C, NP_LOCAL * KMAX), bf16),
             pltpu.VMEM((384, NP_LOCAL * KMAX), bf16),
-            pltpu.SemaphoreType.DMA((7,)),
-            pltpu.SemaphoreType.DMA((7,)),
+            pltpu.SemaphoreType.DMA((6,)),
+            pltpu.SemaphoreType.DMA((6,)),
+            pltpu.SemaphoreType.DMA((16,)),
         ],
-        compiler_params=pltpu.CompilerParams(collective_id=0, has_side_effects=True),
+        compiler_params=pltpu.CompilerParams(
+            collective_id=0, has_side_effects=True
+        ),
         name="cycle",
-    )(facets, taper, kernel, observed, patch_pos, counts, vis_u, vis_v, *tables())
+    )(facets, taper, *tables(), kernel[None], observed, patch_pos, counts, vis_u, vis_v)
     return residual, returned.reshape(2, C, 1, C)
 
 

time: 58.3 us -> 52.7 us (0.904)
  Pallas kernels: 54.6 us -> 50.7 us
  local copies, waits for them, and re-layouts: 2.8 us -> 1.24 us
    pallas_call x1, Pallas kernels: 54.6 us -> 50.7 us  [local(): pl.pallas_call(body, out_shape=(pltpu.VMEM((2, 1, NP_LOCAL, KMAX), f32),...]
    unnamed x2, local copies, waits for them, and re-layouts: 2.8 us -> 1.24 us
where the time goes in v2:
time: 52.7 us; the launch traced here: 52.6 us
  Pallas kernels  50.7 us (96%)
  local copies, waits for them, and re-layouts  1.24 us (2%)
  between operations  0.64 us (1%)
    pallas_call x1, Pallas kernels, local(): pl.pallas_call(body, out_shape=(pltpu.VMEM((2, 1, NP_LOCAL, KMAX), f32),...  50.7 us
    unnamed x2, local copies, waits for them, and re-layouts  1.24 us

profile of v2, /device:TPU:1, one launch (start us, length us, event | category | flops | bytes accessed | tf_op | source)
XLA Modules:
  0.0 52.6 jit_solution(8053806152345173226)
XLA Ops:
  0.6 50.7 %cycle.1 = (f32[2,1,4,512]{3,2,1,0:T(4,128)S(1)}, bf16[2,128,128]{2,1,0:T(8,128)(2,1)S(1)}) custom-call(bf16[1,2,32,4096]{3,2,1,0:T(8,128)(2,1)} %facets_far.1, f32[1,4096]{1,0:T(1,128)} %taper_far.1, bf16[128,256]{1,0:T(8,128)(2,1)} %constant.10.clone.near_far, f32[32,256]{1,0:T(8,128)} %constant.11.clone.far_far, ...), custom_call_target="tpu_custom_call" | custom-call | tf_op jit(solution)/shard_map/cycle/pallas_call | solution.py:371
  51.3 0.6 %copy.18 = f32[2,1,4,512]{3,2,1,0:T(4,128)} copy(f32[2,1,4,512]{3,2,1,0:T(4,128)S(1)} %get-tuple-element.8) | data formatting | bytes 32768
  52.0 0.6 %copy.19 = bf16[2,128,1,128]{3,1,2,0:T(8,128)(2,1)} copy(bf16[2,128,1,128]{3,1,2,0:T(8,128)(2,1)S(1)} %bitcast.4) | data formatting | bytes 131072

commit v3 on v2

--- a/solution.py
+++ b/solution.py
@@ -64,15 +64,6 @@
     return lax.dot_general(left, right, (((1,), (1,)), ((), ())), preferred_element_type=f32)
 
 
-def put_rows(ref, value):
-    for i in range(value.shape[0]):
-        ref[i, 0:1, :] = value[i : i + 1, :]
-
-
-def get_rows(ref):
-    return ref[...].reshape(ref.shape[0], ref.shape[2])
-
-
 def body(
     facets_far, taper_far, near_far, far_far, first_far, twist_far, second_far,
     taps_far, observed_far, patch_pos_far, counts_far, vis_u_far, vis_v_far,
@@ -80,7 +71,7 @@
     facets, taper, near, far, first, twist, second,
     taps, observed, patch_pos, counts, vis_u, vis_v,
     x_out, x_in, q_out, q_in, q_all, u_all, u_out, s_in,
-    y_out, y_in, z_out, z_in, f_out, f_in,
+    y_out, y_in, z_all, z_out, z_in,
     ku, ku_low, kv, kv_wide, weights,
     sent, got, loaded,
 ):
@@ -326,43 +317,42 @@
     total = y_in[0].astype(f32)
     for r in range(1, REPS):
         total = total + y_in[r].astype(f32)
-    put_rows(z_out, total)
-    keep(z_out.at[grp], z_in.at[grp], 4)
+    z_all[pl.ds(3, GRPS, stride=4), :] = jnp.zeros((GRPS, 128), f32)
+    for k in range(3):
+        z_all[pl.ds(k, GRPS, stride=4), :] = total[:, 128 * k : 128 * k + 128]
+    for k in range(GRPS):
+        z_out[k] = z_all[4 * k : 4 * k + 4, :].astype(bf16)
+    keep(z_out.at[grp], z_in.at[sub], 4)
 
     def send_owner(i, _):
         to = grp_peer(i)
-        push(z_out.at[to], z_in.at[grp], 4, (role, to, rep))
+        for k in range(ROLES):
+            push(z_out.at[to], z_in.at[sub], 4, (lax.rem(role + k, ROLES), to, rep))
         return 0
 
     lax.fori_loop(FAR, GRPS, send_owner, 0)
     lax.fori_loop(1, FAR, send_owner, 0)
+    for k in range(1, ROLES):
+        push(z_out.at[grp], z_in.at[sub], 4, (lax.rem(role + k, ROLES), grp, rep))
     arrive(z_in, 4)
-    f_out[0] = get_rows(z_in).astype(bf16)
-    keep(f_out.at[0], f_in.at[role], 5)
-
-    def send_owned(i, _):
-        push(f_out.at[0], f_in.at[role], 5, (lax.rem(role + i, ROLES), grp, rep))
-        return 0
-
-    lax.fori_loop(1, ROLES, send_owned, 0)
-    arrive(f_in, 5)
-
-    owned = jnp.concatenate([f_in[k] for k in range(ROLES)], axis=0).astype(f32)
-    edges = owned[:, 256:]
+
+    for k in range(C):
+        z_all[4 * k : 4 * k + 4, :] = z_in[k].astype(f32)
+    owned = [z_all[pl.ds(k, C, stride=4), :] for k in range(3)]
+    edges = owned[2]
     column = lax.broadcasted_iota(jnp.int32, (C, 128), 1)
     subgrid = lax.broadcasted_iota(jnp.int32, (C, 128), 0)
     for c in range(2):
         side = pltpu.roll(edges, 96 if c == 0 else 32, 1)
         from_left = jnp.where((column < 32) & (subgrid > 0), pltpu.roll(side, 1, 0), 0.0)
         from_right = jnp.where((column >= 96) & (subgrid < C - 1), pltpu.roll(side, C - 1, 0), 0.0)
-        returned[c] = (owned[:, 128 * c : 128 * c + 128] + from_left + from_right).astype(bf16)
+        returned[c] = (owned[c] + from_left + from_right).astype(bf16)
 
     drain(x_in, NEAR - 1, 0)
     drain(q_in, GRPS - 1, 1)
     drain(s_in, NEAR - 1, 2)
     drain(y_in, REPS - 1, 3)
-    drain(z_in, GRPS - 1, 4)
-    drain(f_in, ROLES - 1, 5)
+    drain(z_in, C - 1, 4)
 
 
 def local(facets, taper, kernel, observed, patch_pos, counts, vis_u, vis_v):
@@ -400,17 +390,16 @@
             pltpu.VMEM((NEAR, 8, 256), bf16),
             pltpu.VMEM((REPS, 32, 384), bf16),
             pltpu.VMEM((REPS, 32, 384), bf16),
-            pltpu.VMEM((GRPS, 1, 384), f32),
-            pltpu.VMEM((GRPS, 1, 384), f32),
-            pltpu.VMEM((1, 32, 384), bf16),
-            pltpu.VMEM((ROLES, 32, 384), bf16),
+            pltpu.VMEM((4 * C, 128), f32),
+            pltpu.VMEM((GRPS, 4, 128), bf16),
+            pltpu.VMEM((C, 4, 128), bf16),
             pltpu.VMEM((C, NP_LOCAL * KMAX), f32),
             pltpu.VMEM((C, NP_LOCAL * KMAX), bf16),
             pltpu.VMEM((PATCH, NP_LOCAL * KMAX), f32),
             pltpu.VMEM((C, NP_LOCAL * KMAX), bf16),
             pltpu.VMEM((384, NP_LOCAL * KMAX), bf16),
-            pltpu.SemaphoreType.DMA((6,)),
-            pltpu.SemaphoreType.DMA((6,)),
+            pltpu.SemaphoreType.DMA((5,)),
+            pltpu.SemaphoreType.DMA((5,)),
             pltpu.SemaphoreType.DMA((16,)),
         ],
         compiler_params=pltpu.CompilerParams(

time: 52.7 us -> 50.5 us (0.958)
  Pallas kernels: 50.7 us -> 48.5 us
    pallas_call x1, Pallas kernels: 50.7 us -> 48.5 us  [local(): pl.pallas_call(body, out_shape=(pltpu.VMEM((2, 1, NP_LOCAL, KMAX), f32),...]
where the time goes in v3:
time: 50.5 us; the launch traced here: 50.3 us
  Pallas kernels  48.5 us (96%)
  local copies, waits for them, and re-layouts  1.24 us (2%)
  between operations  0.64 us (1%)
    pallas_call x1, Pallas kernels, local(): pl.pallas_call(body, out_shape=(pltpu.VMEM((2, 1, NP_LOCAL, KMAX), f32),...  48.5 us
    unnamed x2, local copies, waits for them, and re-layouts  1.24 us

profile of v3, /device:TPU:1, one launch (start us, length us, event | category | flops | bytes accessed | tf_op | source)
XLA Modules:
  0.0 50.3 jit_solution(9064996350738179011)
XLA Ops:
  0.6 48.5 %cycle.1 = (f32[2,1,4,512]{3,2,1,0:T(4,128)S(1)}, bf16[2,128,128]{2,1,0:T(8,128)(2,1)S(1)}) custom-call(bf16[1,2,32,4096]{3,2,1,0:T(8,128)(2,1)} %facets_far.1, f32[1,4096]{1,0:T(1,128)} %taper_far.1, bf16[128,256]{1,0:T(8,128)(2,1)} %constant.10.clone.near_far, f32[32,256]{1,0:T(8,128)} %constant.11.clone.far_far, ...), custom_call_target="tpu_custom_call" | custom-call | tf_op jit(solution)/shard_map/cycle/pallas_call | solution.py:361
  49.1 0.6 %copy.18 = f32[2,1,4,512]{3,2,1,0:T(4,128)} copy(f32[2,1,4,512]{3,2,1,0:T(4,128)S(1)} %get-tuple-element.8) | data formatting | bytes 32768
  49.7 0.6 %copy.19 = bf16[2,128,1,128]{3,1,2,0:T(8,128)(2,1)} copy(bf16[2,128,1,128]{3,1,2,0:T(8,128)(2,1)S(1)} %bitcast.4) | data formatting | bytes 131072

commit v4 on v3

--- a/solution.py
+++ b/solution.py
@@ -18,7 +18,6 @@
 GRPS = 32
 REPS = 4
 NEAR = ROLES * REPS
-FAR = 13
 MESH = pl.DeviceIdType.MESH
 bf16 = jnp.bfloat16
 f32 = jnp.float32
@@ -71,8 +70,8 @@
     facets, taper, near, far, first, twist, second,
     taps, observed, patch_pos, counts, vis_u, vis_v,
     x_out, x_in, q_out, q_in, q_all, u_all, u_out, s_in,
-    y_out, y_in, z_all, z_out, z_in,
-    ku, ku_low, kv, kv_wide, weights,
+    z_all, z_out, z_in, s_all, left,
+    ku, kv, kv_wide,
     sent, got, loaded,
 ):
     role, grp, rep = lax.axis_index("role"), lax.axis_index("grp"), lax.axis_index("rep")
@@ -83,11 +82,27 @@
     def grp_peer(i):
         return lax.rem(grp + i, GRPS)
 
+    def for_grps(send):
+        for dz in (2, 1, 3):
+            base = lax.rem(grp // 8 + dz, 4) * 8
+
+            def step(i, _, base=base):
+                send(base + lax.rem(grp + i, 8))
+                return 0
+
+            lax.fori_loop(3, 11, step, 0)
+
+        def last(i, _):
+            send((grp // 8) * 8 + lax.rem(grp + 1 + lax.rem(i, 7), 8))
+            return 0
+
+        lax.fori_loop(2, 9, last, 0)
+
     inputs = [
         (taper_far, taper), (near_far, near), (far_far, far),
-        (first_far, first), (twist_far, twist), (second_far, second),
-        (taps_far, taps), (observed_far, observed), (patch_pos_far, patch_pos),
-        (counts_far, counts), (vis_u_far, vis_u), (vis_v_far, vis_v),
+        (first_far, first), (twist_far, twist), (second_far, second), (taps_far, taps),
+        (observed_far, observed.at[rep]), (patch_pos_far, patch_pos.at[rep]),
+        (counts_far, counts.at[rep]), (vis_u_far, vis_u.at[rep]), (vis_v_far, vis_v.at[rep]),
     ]
     loads = []
     for k in range(4):
@@ -193,23 +208,33 @@
     q_out[0] = jnp.concatenate([cell_re, cell_im], axis=1).astype(bf16)
     keep(q_out.at[0], q_in.at[grp], 1)
 
-    def send_cells(i, _):
-        push(q_out.at[0], q_in.at[grp], 1, (role, grp_peer(i), rep))
-        return 0
-
-    lax.fori_loop(FAR, GRPS, send_cells, 0)
-    lax.fori_loop(1, FAR, send_cells, 0)
+    def send_cells(to):
+        push(q_out.at[0], q_in.at[grp], 1, (role, to, rep))
+
+    for_grps(send_cells)
 
     for load in loads[7:]:
         load.wait()
+    shared = (observed, patch_pos, counts, vis_u, vis_v)
+    for k, held in enumerate(shared):
+
+        def send_held(i, _, held=held, k=k):
+            push(held.at[rep], held.at[rep], 4 + k, (role, grp, lax.rem(rep + i, REPS)))
+            return 0
+
+        lax.fori_loop(1, REPS, send_held, 0)
+    for k, held in enumerate(shared):
+        part = held.at[pl.ds(0, REPS - 1)]
+        pltpu.make_async_copy(part, part, got.at[4 + k]).wait()
+
     sub = role * GRPS + grp
     place = lax.broadcasted_iota(jnp.int32, (PATCH, KMAX), 0)
     row_in_patch = 4 * (place % 8) + place // 8
     has_left = jnp.where(sub > 0, 1, 0)
     has_right = jnp.where(sub < ROLES * GRPS - 1, 1, 0)
 
-    def block_of(p):
-        position = jnp.broadcast_to(patch_pos[0:1, p : p + 1], (1, KMAX))
+    def block_of(k, p, width):
+        position = jnp.broadcast_to(patch_pos[k, 0:1, p : p + 1], (1, width))
         row_block = (
             jnp.where(position >= 6, 1, 0)
             + jnp.where(position >= 12, 1, 0)
@@ -217,27 +242,20 @@
         )
         return row_block, position - 6 * row_block
 
+    patches = [(k, p) for k in range(REPS) for p in range(NP_LOCAL)]
     tap = [jnp.broadcast_to(taps[0:1, t : t + 1], (PATCH, KMAX)) for t in range(KW)]
-    for p in range(NP_LOCAL):
-        cols = slice(KMAX * p, KMAX * p + KMAX)
-        row_block, col_block = block_of(p)
-        du = row_in_patch - vis_u[0, p : p + 1, :]
-        dv = place - vis_v[0, p : p + 1, :]
+    for k, p in patches:
+        cols = slice(KMAX * (NP_LOCAL * k + p), KMAX * (NP_LOCAL * k + p + 1))
+        _, col_block = block_of(k, p, KMAX)
+        du = row_in_patch - vis_u[k, 0, p : p + 1, :]
+        dv = place - vis_v[k, 0, p : p + 1, :]
         u32 = jnp.zeros((PATCH, KMAX), f32)
         v32 = jnp.zeros((PATCH, KMAX), f32)
         for t in range(KW):
             u32 = jnp.where(du == t, tap[t], u32)
             v32 = jnp.where(dv == t, tap[t], v32)
+        ku[:, cols] = u32
         kv[:, cols] = v32
-        for r in range(REPS):
-            rows = u32[8 * r : 8 * r + 8]
-            for h in range(2):
-                pair = jnp.concatenate(
-                    [jnp.where(row_block == 2 * h + k, rows, 0.0) for k in range(2)], axis=0
-                )
-                at = slice(32 * r + 16 * h, 32 * r + 16 * h + 16)
-                ku[at, cols] = pair
-                ku_low[at, cols] = pair.astype(bf16)
         for u in range(4):
             chosen = jnp.where(col_block == u + 1, 1, 0)
             if u == 2:
@@ -279,62 +297,65 @@
     lax.fori_loop(1, NEAR, send_rows, 0)
     arrive(s_in, 2)
 
-    rows = jnp.concatenate([s_in[k].astype(f32) for k in range(NEAR)], axis=0).astype(bf16)
-    grid_cells = jnp.concatenate([rows[:, :128], rows[:, 128:]], axis=0)
+    for k in range(NEAR):
+        arrived = s_in[k].astype(f32)
+        for c in range(2):
+            s_all[128 * c + 8 * k : 128 * c + 8 * k + 8, :] = arrived[:, 128 * c : 128 * c + 128]
     slots = lax.broadcasted_iota(jnp.int32, (1, KMAX), 1)
-    for p in range(NP_LOCAL):
-        cols = slice(KMAX * p, KMAX * p + KMAX)
-        _, col_block = block_of(p)
-        live = slots < jnp.broadcast_to(counts[0:1, p : p + 1], (1, KMAX))
-        along = mm(grid_cells, kv_wide[:, cols])
+    total = [[jnp.zeros((8, 128), f32) for _ in range(4)] for _ in range(3)]
+    for k, p in patches:
+        cols = slice(KMAX * (NP_LOCAL * k + p), KMAX * (NP_LOCAL * k + p + 1))
+        row_block, col_block = block_of(k, p, 128)
+        rows = []
+        for m in range(8):
+            block = s_all[32 * m : 32 * m + 8, :]
+            for h in range(1, 4):
+                at = slice(32 * m + 8 * h, 32 * m + 8 * h + 8)
+                block = jnp.where(row_block == h, s_all[at, :], block)
+            rows.append(block)
+        along = mm(jnp.concatenate(rows, axis=0).astype(bf16), kv_wide[:, cols])
+        live = slots < jnp.broadcast_to(counts[k, 0:1, p : p + 1], (1, KMAX))
         ku_p = ku[:, cols]
         kv_p = kv[:, cols]
+        weighted = []
         for c in range(2):
-            predicted = jnp.sum(along[128 * c : 128 * c + 128] * ku_p, axis=0, keepdims=True)
-            left_over = jnp.where(live, observed[c, 0, p : p + 1, :] - predicted, 0.0)
-            residual[c, 0, p : p + 1, :] = left_over
-            weighted = kv_p * left_over
-            for u in range(4):
-                at = slice(128 * c + 32 * u, 128 * c + 32 * u + 32)
-                weights[at, cols] = jnp.where(col_block == u + 1, weighted, 0.0).astype(bf16)
-            at = slice(256 + 64 * c, 256 + 64 * c + 32)
-            weights[at, cols] = jnp.where(col_block == 0, weighted, 0.0).astype(bf16)
-            at = slice(288 + 64 * c, 288 + 64 * c + 32)
-            weights[at, cols] = jnp.where(col_block == 5, weighted, 0.0).astype(bf16)
-    gridded = mm_t(ku_low[...], weights[...])
-    for r in range(REPS):
-        y_out[r] = gridded[32 * r : 32 * r + 32].astype(bf16)
-
-    keep(y_out.at[rep], y_in.at[rep], 3)
-
-    def send_gridded(i, _):
-        to = lax.rem(rep + i, REPS)
-        push(y_out.at[to], y_in.at[rep], 3, (role, grp, to))
-        return 0
-
-    lax.fori_loop(1, REPS, send_gridded, 0)
-    arrive(y_in, 3)
-    total = y_in[0].astype(f32)
-    for r in range(1, REPS):
-        total = total + y_in[r].astype(f32)
+            predicted = jnp.sum(along[32 * c : 32 * c + 32] * ku_p, axis=0, keepdims=True)
+            left_over = jnp.where(live, observed[k, c, 0, p : p + 1, :] - predicted, 0.0)
+            left[k, c, 0, p : p + 1, :] = left_over
+            weighted.append((kv_p * left_over).astype(bf16))
+        mine_u = ku[pl.ds(pl.multiple_of(8 * rep, 8), 8), cols].astype(bf16)
+        both = mm_t(mine_u, jnp.concatenate(weighted + weighted, axis=0))
+        turned = pltpu.roll(both, 32, 1)
+        even = (lane // 32) % 2 == 0
+        pieces = (
+            (jnp.where(even, both, turned), lane // 32 == col_block - 1),
+            (jnp.where(even, turned, both), lane // 32 == col_block - 1),
+            (
+                jnp.where((lane < 32) | (lane >= 96), both, turned),
+                jnp.where(even, 0, 5) == col_block,
+            ),
+        )
+        for j, (piece, inside) in enumerate(pieces):
+            for h in range(4):
+                here = jnp.where(row_block == h, 1, 0) * jnp.where(inside, 1, 0)
+                total[j][h] = total[j][h] + jnp.where(here > 0, piece, 0.0)
+
     z_all[pl.ds(3, GRPS, stride=4), :] = jnp.zeros((GRPS, 128), f32)
     for k in range(3):
-        z_all[pl.ds(k, GRPS, stride=4), :] = total[:, 128 * k : 128 * k + 128]
+        z_all[pl.ds(k, GRPS, stride=4), :] = jnp.concatenate(total[k], axis=0)
     for k in range(GRPS):
         z_out[k] = z_all[4 * k : 4 * k + 4, :].astype(bf16)
-    keep(z_out.at[grp], z_in.at[sub], 4)
-
-    def send_owner(i, _):
-        to = grp_peer(i)
+    keep(z_out.at[grp], z_in.at[sub], 3)
+
+    def send_owner(to):
         for k in range(ROLES):
-            push(z_out.at[to], z_in.at[sub], 4, (lax.rem(role + k, ROLES), to, rep))
-        return 0
-
-    lax.fori_loop(FAR, GRPS, send_owner, 0)
-    lax.fori_loop(1, FAR, send_owner, 0)
+            push(z_out.at[to], z_in.at[sub], 3, (lax.rem(role + k, ROLES), to, rep))
+
+    for_grps(send_owner)
     for k in range(1, ROLES):
-        push(z_out.at[grp], z_in.at[sub], 4, (lax.rem(role + k, ROLES), grp, rep))
-    arrive(z_in, 4)
+        push(z_out.at[grp], z_in.at[sub], 3, (lax.rem(role + k, ROLES), grp, rep))
+    residual[...] = left[rep]
+    arrive(z_in, 3)
 
     for k in range(C):
         z_all[4 * k : 4 * k + 4, :] = z_in[k].astype(f32)
@@ -351,8 +372,20 @@
     drain(x_in, NEAR - 1, 0)
     drain(q_in, GRPS - 1, 1)
     drain(s_in, NEAR - 1, 2)
-    drain(y_in, REPS - 1, 3)
-    drain(z_in, C - 1, 4)
+    drain(z_in, C - 1, 3)
+    for k, held in enumerate(shared):
+        drain(held, REPS - 1, 4 + k)
+
+
+def flush(residual, returned, residual_out, returned_out, done):
+    copies = [
+        pltpu.make_async_copy(returned, returned_out, done.at[0]),
+        pltpu.make_async_copy(residual, residual_out, done.at[1]),
+    ]
+    for copy in copies:
+        copy.start()
+    for copy in copies:
+        copy.wait()
 
 
 def local(facets, taper, kernel, observed, patch_pos, counts, vis_u, vis_v):
@@ -375,11 +408,11 @@
             pltpu.VMEM((128, 256), f32),
             pltpu.VMEM((GRPS, 8, 256), bf16),
             pltpu.VMEM((1, KW), f32),
-            pltpu.VMEM((2, 1, NP_LOCAL, KMAX), f32),
-            pltpu.VMEM((1, NP_LOCAL), jnp.int32),
-            pltpu.VMEM((1, NP_LOCAL), jnp.int32),
-            pltpu.VMEM((1, NP_LOCAL, KMAX), jnp.int32),
-            pltpu.VMEM((1, NP_LOCAL, KMAX), jnp.int32),
+            pltpu.VMEM((REPS, 2, 1, NP_LOCAL, KMAX), f32),
+            pltpu.VMEM((REPS, 1, NP_LOCAL), jnp.int32),
+            pltpu.VMEM((REPS, 1, NP_LOCAL), jnp.int32),
+            pltpu.VMEM((REPS, 1, NP_LOCAL, KMAX), jnp.int32),
+            pltpu.VMEM((REPS, 1, NP_LOCAL, KMAX), jnp.int32),
             pltpu.VMEM((NEAR, 8, 128), bf16),
             pltpu.VMEM((NEAR, 8, 128), bf16),
             pltpu.VMEM((1, 8, 256), bf16),
@@ -388,18 +421,16 @@
             pltpu.VMEM((64, 128), f32),
             pltpu.VMEM((ROLES, 8, 256), bf16),
             pltpu.VMEM((NEAR, 8, 256), bf16),
-            pltpu.VMEM((REPS, 32, 384), bf16),
-            pltpu.VMEM((REPS, 32, 384), bf16),
             pltpu.VMEM((4 * C, 128), f32),
             pltpu.VMEM((GRPS, 4, 128), bf16),
             pltpu.VMEM((C, 4, 128), bf16),
-            pltpu.VMEM((C, NP_LOCAL * KMAX), f32),
-            pltpu.VMEM((C, NP_LOCAL * KMAX), bf16),
-            pltpu.VMEM((PATCH, NP_LOCAL * KMAX), f32),
-            pltpu.VMEM((C, NP_LOCAL * KMAX), bf16),
-            pltpu.VMEM((384, NP_LOCAL * KMAX), bf16),
-            pltpu.SemaphoreType.DMA((5,)),
-            pltpu.SemaphoreType.DMA((5,)),
+            pltpu.VMEM((2 * C, 128), f32),
+            pltpu.VMEM((REPS, 2, 1, NP_LOCAL, KMAX), f32),
+            pltpu.VMEM((PATCH, REPS * NP_LOCAL * KMAX), f32),
+            pltpu.VMEM((PATCH, REPS * NP_LOCAL * KMAX), f32),
+            pltpu.VMEM((C, REPS * NP_LOCAL * KMAX), bf16),
+            pltpu.SemaphoreType.DMA((9,)),
+            pltpu.SemaphoreType.DMA((9,)),
             pltpu.SemaphoreType.DMA((16,)),
         ],
         compiler_params=pltpu.CompilerParams(
@@ -407,6 +438,19 @@
         ),
         name="cycle",
     )(facets, taper, *tables(), kernel[None], observed, patch_pos, counts, vis_u, vis_v)
+    anywhere = pl.BlockSpec(memory_space=pl.ANY)
+    residual, returned = pl.pallas_call(
+        flush,
+        out_shape=(
+            jax.ShapeDtypeStruct((2, 1, NP_LOCAL, KMAX), f32),
+            jax.ShapeDtypeStruct((2, C, C), bf16),
+        ),
+        in_specs=[vmem, vmem],
+        out_specs=(anywhere, anywhere),
+        scratch_shapes=[pltpu.SemaphoreType.DMA((2,))],
+        compiler_params=pltpu.CompilerParams(vmem_limit_bytes=1 << 20),
+        name="flush",
+    )(residual, returned)
     return residual, returned.reshape(2, C, 1, C)
 
 

time: 50.5 us -> 45.2 us (0.90)
  Pallas kernels: 48.5 us -> 44.5 us
  local copies, waits for them, and re-layouts: 1.24 us -> 0 us
    pallas_call x1, Pallas kernels: 48.5 us -> 43.8 us  [local(): pl.pallas_call(body, out_shape=(pltpu.VMEM((2, 1, NP_LOCAL, KMAX), f32),...]
    unnamed x2 -> x0, local copies, waits for them, and re-layouts: 1.24 us -> none
    pallas_call x0 -> x1, Pallas kernels: none -> 0.65 us  [local(): pl.pallas_call(flush, out_shape=(jax.ShapeDtypeStruct((2, 1, NP_LOCAL, KM...]
where the time goes in v4:
time: 45.2 us; the launch traced here: 45.1 us
  Pallas kernels  44.5 us (98%)
  between operations  0.64 us (1%)
    pallas_call x1, Pallas kernels, local(): pl.pallas_call(body, out_shape=(pltpu.VMEM((2, 1, NP_LOCAL, KMAX), f32),...  43.8 us

profile of v4, /device:TPU:1, one launch (start us, length us, event | category | flops | bytes accessed | tf_op | source)
XLA Modules:
  0.0 45.1 jit_solution(6733826616460345170)
XLA Ops:
  0.6 43.8 %cycle.1 = (f32[2,1,4,512]{3,2,1,0:T(4,128)S(1)}, bf16[2,128,128]{2,1,0:T(8,128)(2,1)S(1)}) custom-call(bf16[1,2,32,4096]{3,2,1,0:T(8,128)(2,1)} %facets_far.1, f32[1,4096]{1,0:T(1,128)} %taper_far.1, bf16[128,256]{1,0:T(8,128)(2,1)} %constant.10.clone.near_far, f32[32,256]{1,0:T(8,128)} %constant.11.clone.far_far, ...), custom_call_target="tpu_custom_call" | custom-call | tf_op jit(solution)/shard_map/cycle/pallas_call | solution.py:394
  44.5 0.7 %flush.1 = (f32[2,1,4,512]{3,2,1,0:T(4,128)}, bf16[2,128,128]{2,1,0:T(8,128)(2,1)}) custom-call(f32[2,1,4,512]{3,2,1,0:T(4,128)S(1)} %get-tuple-element.6.residual, bf16[2,128,128]{2,1,0:T(8,128)(2,1)S(1)} %get-tuple-element.7.returned), custom_call_target="tpu_custom_call" | custom-call | tf_op jit(solution)/shard_map/flush/pallas_call | solution.py:442

commit v5 on v4

--- a/solution.py
+++ b/solution.py
@@ -143,13 +143,12 @@
         part = buffer.at[pl.ds(0, count)]
         pltpu.make_async_copy(part, part, sent.at[phase]).wait()
 
-    for load in loads[4:7]:
+    for load in loads[:7]:
         load.wait()
     table = near[...]
     part_re = jnp.zeros((32, C), f32)
     part_im = jnp.zeros((32, C), f32)
     for chunk in range(4):
-        loads[chunk].wait()
         blocks = []
         for i in range(8 * chunk, 8 * chunk + 8):
             at = slice(128 * i, 128 * i + 128)
@@ -351,9 +350,18 @@
         for k in range(ROLES):
             push(z_out.at[to], z_in.at[sub], 3, (lax.rem(role + k, ROLES), to, rep))
 
-    for_grps(send_owner)
-    for k in range(1, ROLES):
-        push(z_out.at[grp], z_in.at[sub], 3, (lax.rem(role + k, ROLES), grp, rep))
+    def send_early(i, _):
+        to = i
+
+        @pl.when(to != grp)
+        def _():
+            push(z_out.at[to], z_in.at[sub], 3, (role, to, rep))
+
+        for k in range(1, ROLES):
+            push(z_out.at[to], z_in.at[sub], 3, (lax.rem(role + k, ROLES), to, rep))
+        return 0
+
+    lax.fori_loop(0, GRPS, send_early, 0)
     residual[...] = left[rep]
     arrive(z_in, 3)
 

time: 45.2 us -> 44.6 us (0.987)
  Pallas kernels: 44.5 us -> 43.8 us
    pallas_call x1, Pallas kernels: 43.8 us -> 43.2 us  [local(): pl.pallas_call(body, out_shape=(pltpu.VMEM((2, 1, NP_LOCAL, KMAX), f32),...]
where the time goes in v5:
time: 44.6 us; the launch traced here: 44.5 us
  Pallas kernels  43.8 us (98%)
  between operations  0.64 us (1%)
    pallas_call x1, Pallas kernels, local(): pl.pallas_call(body, out_shape=(pltpu.VMEM((2, 1, NP_LOCAL, KMAX), f32),...  43.2 us

profile of v5, /device:TPU:1, one launch (start us, length us, event | category | flops | bytes accessed | tf_op | source)
XLA Modules:
  0.0 44.5 jit_solution(17268921519993605068)
XLA Ops:
  0.6 43.2 %cycle.1 = (f32[2,1,4,512]{3,2,1,0:T(4,128)S(1)}, bf16[2,128,128]{2,1,0:T(8,128)(2,1)S(1)}) custom-call(bf16[1,2,32,4096]{3,2,1,0:T(8,128)(2,1)} %facets_far.1, f32[1,4096]{1,0:T(1,128)} %taper_far.1, bf16[128,256]{1,0:T(8,128)(2,1)} %constant.10.clone.near_far, f32[32,256]{1,0:T(8,128)} %constant.11.clone.far_far, ...), custom_call_target="tpu_custom_call" | custom-call | tf_op jit(solution)/shard_map/cycle/pallas_call | solution.py:402
  43.8 0.7 %flush.1 = (f32[2,1,4,512]{3,2,1,0:T(4,128)}, bf16[2,128,128]{2,1,0:T(8,128)(2,1)}) custom-call(f32[2,1,4,512]{3,2,1,0:T(4,128)S(1)} %get-tuple-element.6.residual, bf16[2,128,128]{2,1,0:T(8,128)(2,1)S(1)} %get-tuple-element.7.returned), custom_call_target="tpu_custom_call" | custom-call | tf_op jit(solution)/shard_map/flush/pallas_call | solution.py:450

commit v6 on v5

--- a/solution.py
+++ b/solution.py
@@ -302,26 +302,36 @@
             s_all[128 * c + 8 * k : 128 * c + 8 * k + 8, :] = arrived[:, 128 * c : 128 * c + 128]
     slots = lax.broadcasted_iota(jnp.int32, (1, KMAX), 1)
     total = [[jnp.zeros((8, 128), f32) for _ in range(4)] for _ in range(3)]
+    def columns(k, p):
+        return slice(KMAX * (NP_LOCAL * k + p), KMAX * (NP_LOCAL * k + p + 1))
+
+    for k in range(REPS):
+        predicted = [[], []]
+        live = []
+        for p in range(NP_LOCAL):
+            row_block, _ = block_of(k, p, 128)
+            rows = []
+            for m in range(8):
+                block = s_all[32 * m : 32 * m + 8, :]
+                for h in range(1, 4):
+                    at = slice(32 * m + 8 * h, 32 * m + 8 * h + 8)
+                    block = jnp.where(row_block == h, s_all[at, :], block)
+                rows.append(block)
+            along = mm(jnp.concatenate(rows, axis=0).astype(bf16), kv_wide[:, columns(k, p)])
+            ku_p = ku[:, columns(k, p)]
+            for c in range(2):
+                product = along[32 * c : 32 * c + 32] * ku_p
+                predicted[c].append(jnp.sum(product, axis=0, keepdims=True))
+            live.append(jnp.broadcast_to(counts[k, 0:1, p : p + 1], (1, KMAX)))
+        alive = slots < jnp.concatenate(live, axis=0)
+        for c in range(2):
+            over = observed[k, c, 0] - jnp.concatenate(predicted[c], axis=0)
+            left[k, c, 0] = jnp.where(alive, over, 0.0)
     for k, p in patches:
-        cols = slice(KMAX * (NP_LOCAL * k + p), KMAX * (NP_LOCAL * k + p + 1))
+        cols = columns(k, p)
         row_block, col_block = block_of(k, p, 128)
-        rows = []
-        for m in range(8):
-            block = s_all[32 * m : 32 * m + 8, :]
-            for h in range(1, 4):
-                at = slice(32 * m + 8 * h, 32 * m + 8 * h + 8)
-                block = jnp.where(row_block == h, s_all[at, :], block)
-            rows.append(block)
-        along = mm(jnp.concatenate(rows, axis=0).astype(bf16), kv_wide[:, cols])
-        live = slots < jnp.broadcast_to(counts[k, 0:1, p : p + 1], (1, KMAX))
-        ku_p = ku[:, cols]
         kv_p = kv[:, cols]
-        weighted = []
-        for c in range(2):
-            predicted = jnp.sum(along[32 * c : 32 * c + 32] * ku_p, axis=0, keepdims=True)
-            left_over = jnp.where(live, observed[k, c, 0, p : p + 1, :] - predicted, 0.0)
-            left[k, c, 0, p : p + 1, :] = left_over
-            weighted.append((kv_p * left_over).astype(bf16))
+        weighted = [(kv_p * left[k, c, 0, p : p + 1, :]).astype(bf16) for c in range(2)]
         mine_u = ku[pl.ds(pl.multiple_of(8 * rep, 8), 8), cols].astype(bf16)
         both = mm_t(mine_u, jnp.concatenate(weighted + weighted, axis=0))
         turned = pltpu.roll(both, 32, 1)

time: 44.6 us -> 43.6 us (0.978)
  Pallas kernels: 43.8 us -> 42.8 us
    pallas_call x1, Pallas kernels: 43.2 us -> 42.1 us  [local(): pl.pallas_call(body, out_shape=(pltpu.VMEM((2, 1, NP_LOCAL, KMAX), f32),...]
where the time goes in v6:
time: 43.6 us; the launch traced here: 43.4 us
  Pallas kernels  42.8 us (98%)
  between operations  0.64 us (1%)
    pallas_call x1, Pallas kernels, local(): pl.pallas_call(body, out_shape=(pltpu.VMEM((2, 1, NP_LOCAL, KMAX), f32),...  42.1 us

profile of v6, /device:TPU:1, one launch (start us, length us, event | category | flops | bytes accessed | tf_op | source)
XLA Modules:
  0.0 43.4 jit_solution(70487813089376839)
XLA Ops:
  0.6 42.1 %cycle.1 = (f32[2,1,4,512]{3,2,1,0:T(4,128)S(1)}, bf16[2,128,128]{2,1,0:T(8,128)(2,1)S(1)}) custom-call(bf16[1,2,32,4096]{3,2,1,0:T(8,128)(2,1)} %facets_far.1, f32[1,4096]{1,0:T(1,128)} %taper_far.1, bf16[128,256]{1,0:T(8,128)(2,1)} %constant.10.clone.near_far, f32[32,256]{1,0:T(8,128)} %constant.11.clone.far_far, ...), custom_call_target="tpu_custom_call" | custom-call | tf_op jit(solution)/shard_map/cycle/pallas_call | solution.py:412
  42.8 0.7 %flush.1 = (f32[2,1,4,512]{3,2,1,0:T(4,128)}, bf16[2,128,128]{2,1,0:T(8,128)(2,1)}) custom-call(f32[2,1,4,512]{3,2,1,0:T(4,128)S(1)} %get-tuple-element.6.residual, bf16[2,128,128]{2,1,0:T(8,128)(2,1)S(1)} %get-tuple-element.7.returned), custom_call_target="tpu_custom_call" | custom-call | tf_op jit(solution)/shard_map/flush/pallas_call | solution.py:460

commit v7 on v6

--- a/solution.py
+++ b/solution.py
@@ -77,7 +77,7 @@
     role, grp, rep = lax.axis_index("role"), lax.axis_index("grp"), lax.axis_index("rep")
 
     def near_peer(i):
-        return (lax.rem(role + i // REPS, ROLES), grp, lax.rem(rep + i % REPS, REPS))
+        return (lax.rem(role + i // REPS + 2, ROLES), grp, lax.rem(rep + i % REPS + 2, REPS))
 
     def grp_peer(i):
         return lax.rem(grp + i, GRPS)
@@ -125,7 +125,8 @@
         return 0
 
     lax.fori_loop(1, GRPS, greet_grp, 0)
-    lax.fori_loop(1, NEAR, greet_near, 0)
+    lax.fori_loop(0, 10, greet_near, 0)
+    lax.fori_loop(11, NEAR, greet_near, 0)
 
     def push(src, dst, phase, device):
         pltpu.make_async_remote_copy(
@@ -190,7 +191,8 @@
             push(out.at[device[0] * REPS + device[2]], into.at[slot], phase, device)
             return 0
 
-        lax.fori_loop(1, NEAR, send, 0)
+        lax.fori_loop(0, 10, send, 0)
+        lax.fori_loop(11, NEAR, send, 0)
 
     spread(x_out, x_in, 0)
     arrive(x_in, 0)
@@ -293,7 +295,8 @@
         push(u_out.at[device[0]], s_in.at[slot], 2, device)
         return 0
 
-    lax.fori_loop(1, NEAR, send_rows, 0)
+    lax.fori_loop(0, 10, send_rows, 0)
+    lax.fori_loop(11, NEAR, send_rows, 0)
     arrive(s_in, 2)
 
     for k in range(NEAR):

time: 43.6 us -> 43.4 us (level)
  no operation moved by 1% of the time
where the time goes in v7:
time: 43.4 us; the launch traced here: 43.3 us
  Pallas kernels  42.6 us (98%)
  between operations  0.64 us (1%)
    pallas_call x1, Pallas kernels, local(): pl.pallas_call(body, out_shape=(pltpu.VMEM((2, 1, NP_LOCAL, KMAX), f32),...  42 us

profile of v7, /device:TPU:1, one launch (start us, length us, event | category | flops | bytes accessed | tf_op | source)
XLA Modules:
  0.0 43.3 jit_solution(4759157579508555930)
XLA Ops:
  0.6 42.0 %cycle.1 = (f32[2,1,4,512]{3,2,1,0:T(4,128)S(1)}, bf16[2,128,128]{2,1,0:T(8,128)(2,1)S(1)}) custom-call(bf16[1,2,32,4096]{3,2,1,0:T(8,128)(2,1)} %facets_far.1, f32[1,4096]{1,0:T(1,128)} %taper_far.1, bf16[128,256]{1,0:T(8,128)(2,1)} %constant.10.clone.near_far, f32[32,256]{1,0:T(8,128)} %constant.11.clone.far_far, ...), custom_call_target="tpu_custom_call" | custom-call | tf_op jit(solution)/shard_map/cycle/pallas_call | solution.py:415
  42.6 0.7 %flush.1 = (f32[2,1,4,512]{3,2,1,0:T(4,128)}, bf16[2,128,128]{2,1,0:T(8,128)(2,1)}) custom-call(f32[2,1,4,512]{3,2,1,0:T(4,128)S(1)} %get-tuple-element.6.residual, bf16[2,128,128]{2,1,0:T(8,128)(2,1)S(1)} %get-tuple-element.7.returned), custom_call_target="tpu_custom_call" | custom-call | tf_op jit(solution)/shard_map/flush/pallas_call | solution.py:463
